TPU v7x, 32 devices: a whole 2x2x4 slice. The times are simulated.
32 devices in a mesh: dp: 4 (over z), shard: 8 (over y, x, core).
Axes of the slice: x: 2, y: 2, z: 4, core: 2. Of those that a mesh axis runs over, the one named last changes fastest.
Arguments:
- token_ids: int32 [64, 1024], P(('dp', 'shard')), may hold values from 0 to 49151
- seq_lengths: int32 [64], P(('dp', 'shard')), may hold values from 256 to 768, as said below
- completion_mask: int32 [64, 1024], P(('dp', 'shard')), may hold values from 0 to 1, as said below
- deal: int32 [64], P(('dp', 'shard')), may hold values from 0 to 15, as said below
- attend_in: float32 [960, 1600], P('shard'), may hold values from -0.1875 to 0.1875
- attend_out: float32 [960, 960], P('shard'), may hold values from -0.25 to 0.25
- feed_in: float32 [960, 5120], P('shard'), may hold values from -0.1875 to 0.1875
- feed_out: float32 [2560, 960], P('shard'), may hold values from -0.046875 to 0.046875
- norm_gains: float32 [3, 960], P(None, 'shard'), may hold values from 0.5 to 1.5
- embed_table: float32 [49152, 960], P(('dp', 'shard')), may hold values from -1 to 1
- attend_in_first: float32 [960, 1600], P('shard'), may hold values from -7.6293945e-06 to 7.6293945e-06
- attend_out_first: float32 [960, 960], P('shard'), may hold values from -7.6293945e-06 to 7.6293945e-06
- feed_in_first: float32 [960, 5120], P('shard'), may hold values from -7.6293945e-06 to 7.6293945e-06
- feed_out_first: float32 [2560, 960], P('shard'), may hold values from -7.6293945e-06 to 7.6293945e-06
- norm_gains_first: float32 [3, 960], P(None, 'shard'), may hold values from -7.6293945e-06 to 7.6293945e-06
- embed_table_first: float32 [49152, 960], P(('dp', 'shard')), may hold values from -7.6293945e-06 to 7.6293945e-06
- attend_in_second: float32 [960, 1600], P('shard'), may hold values from 1.7537952e-12 to 7.015181e-12
- attend_out_second: float32 [960, 960], P('shard'), may hold values from 1.7537952e-12 to 7.015181e-12
- feed_in_second: float32 [960, 5120], P('shard'), may hold values from 1.7537952e-12 to 7.015181e-12
- feed_out_second: float32 [2560, 960], P('shard'), may hold values from 1.7537952e-12 to 7.015181e-12
- norm_gains_second: float32 [3, 960], P(None, 'shard'), may hold values from 1.7537952e-12 to 7.015181e-12
- embed_table_second: float32 [49152, 960], P(('dp', 'shard')), may hold values from 1.7537952e-12 to 7.015181e-12
Outputs:
- new_attend_in: float32 [960, 1600], P('shard')
- new_attend_out: float32 [960, 960], P('shard')
- new_feed_in: float32 [960, 5120], P('shard')
- new_feed_out: float32 [2560, 960], P('shard')
- norm_gains_update: float32 [3, 960], P(None, 'shard')
- new_embed_table: float32 [49152, 960], P(('dp', 'shard'))
- new_attend_in_first: float32 [960, 1600], P('shard')
- new_attend_out_first: float32 [960, 960], P('shard')
- new_feed_in_first: float32 [960, 5120], P('shard')
- new_feed_out_first: float32 [2560, 960], P('shard')
- new_norm_gains_first: float32 [3, 960], P(None, 'shard')
- new_embed_table_first: float32 [49152, 960], P(('dp', 'shard'))
- new_attend_in_second: float32 [960, 1600], P('shard')
- new_attend_out_second: float32 [960, 960], P('shard')
- new_feed_in_second: float32 [960, 5120], P('shard')
- new_feed_out_second: float32 [2560, 960], P('shard')
- new_norm_gains_second: float32 [3, 960], P(None, 'shard')
- new_embed_table_second: float32 [49152, 960], P(('dp', 'shard'))
- mean_loss: float32 [], replicated
- grad_norm: float32 [], replicated
- seq_loss: float32 [64], P(('dp', 'shard'))
Inputs may be any that keep to these rules, and one draw needn't show every extreme that they name: `seq_lengths`: the sequences at packed places 2b and 2b + 1 have lengths summing to exactly 1024; in every draw some sequence has 256 tokens and its partner the rest. `completion_mask`: each input slot holds exactly 16 ones, all at positions t with 1024 - length <= t <= 1022 of that slot's sequence. On the 16 sequences of each index of dp (consecutive in input order), deal is a permutation.
All inputs are finite; a program needn't handle non-finite values.
Results may differ from a plain program's by a relative error of at most 0.009.
The roundings to bfloat16 on the way count: a program that leaves them out, or rounds other values in their place, can miss the bound.
Values may be sent and summed in bfloat16 or wider, within the bound.
A program may use at most 384 MiB of HBM per device.

v0:
```python
import jax
import jax.numpy as jnp
from jax import lax
from jax.sharding import PartitionSpec as P

HEADS = 15
KV_HEADS = 5
HEAD_DIM = 64
COMP = 16
STEP = 3


eps_norm = 1e-05
rope_base = 100000.0
beta_one = 0.5
beta_two = 0.5
adam_eps = 1e-08
learn_rate = 0.008
weight_decay = 0.1
max_norm = 0.01
masked_score = -1e30


def merged(part, axis, combine):
    gathered = jax.tree.map(lambda a: lax.all_gather(a, axis), part)

    def take(source):
        return jax.tree.map(lambda a: lax.dynamic_index_in_dim(a, source, 0, False), gathered)

    return lax.fori_loop(
        1, lax.axis_size(axis), lambda source, state: combine(state, take(source)), take(0)
    )


def contract_last(left, right):
    return lax.dot_general(
        left, right, (((1,), (1,)), ((), ())), preferred_element_type=jnp.float32
    )


def contract_first(left, right):
    return lax.dot_general(
        left, right, (((0,), (0,)), ((), ())), preferred_element_type=jnp.float32
    )


def rms_scale(rows_in):
    return lax.rsqrt(jnp.mean(rows_in * rows_in, axis=-1, keepdims=True) + eps_norm)


def norm_back(rows_in, gain_row, incoming):
    scale_rows = rms_scale(rows_in)
    weighted = incoming * gain_row
    d_rows = scale_rows * weighted - rows_in * (scale_rows * scale_rows * scale_rows) * jnp.mean(
        weighted * rows_in, axis=-1, keepdims=True
    )
    return (d_rows, jnp.sum(incoming * rows_in * scale_rows, axis=0))


def rotation(positions):
    half_dim = HEAD_DIM // 2
    freqs = rope_base ** (-jnp.arange(half_dim, dtype=jnp.float32) * 2.0 / HEAD_DIM)
    angles = positions[:, None] * freqs[None, :]
    return (jnp.cos(angles)[:, None, :], jnp.sin(angles)[:, None, :])


def rotate(rows_in, cos_rows, sin_rows, turn_sign):
    half_dim = rows_in.shape[-1] // 2
    first_half = rows_in[..., :half_dim]
    second_half = rows_in[..., half_dim:]
    return jnp.concatenate(
        [
            first_half * cos_rows - turn_sign * second_half * sin_rows,
            second_half * cos_rows + turn_sign * first_half * sin_rows,
        ],
        axis=-1,
    )


def locate(id_rows, rows_dev, shard_count, shard_me):
    block_id = id_rows // rows_dev
    owned_mask = block_id % shard_count == shard_me
    local_row = block_id // shard_count * rows_dev + id_rows % rows_dev
    return (owned_mask, local_row)


def adamw_update(master, first_old, second_old, gradient, decay_on):
    first_new = beta_one * first_old + (1.0 - beta_one) * gradient
    second_new = beta_two * second_old + (1.0 - beta_two) * gradient * gradient
    first_hat = first_new / (1.0 - beta_one**STEP)
    second_hat = second_new / (1.0 - beta_two**STEP)
    change = -learn_rate * (
        first_hat / (jnp.sqrt(second_hat) + adam_eps) + decay_on * weight_decay * master
    )
    return (master + change, first_new, second_new, change)


def per_device(
    token_ids,
    seq_lengths,
    completion_mask,
    deal,
    attend_in,
    attend_out,
    feed_in,
    feed_out,
    norm_gains,
    embed_table,
    attend_in_first,
    attend_out_first,
    feed_in_first,
    feed_out_first,
    norm_gains_first,
    embed_table_first,
    attend_in_second,
    attend_out_second,
    feed_in_second,
    feed_out_second,
    norm_gains_second,
    embed_table_second,
):
    shard_count = lax.axis_size("shard")
    group_count = lax.axis_size("dp")
    shard_me = lax.axis_index("shard")
    total_rows = 2 * COMP * shard_count * group_count
    masters = (attend_in, attend_out, feed_in, feed_out, norm_gains)
    copies = tuple((master.astype(jnp.bfloat16) for master in masters))
    w_qkv, w_out, w_gate_up, w_down, gain_rows = (
        lax.all_gather(copies[0], "shard", axis=0, tiled=True),
        lax.all_gather(copies[1], "shard", axis=0, tiled=True),
        lax.all_gather(copies[2], "shard", axis=0, tiled=True),
        lax.all_gather(copies[3], "shard", axis=0, tiled=True),
        lax.all_gather(copies[4], "shard", axis=1, tiled=True),
    )
    vocab_slice = lax.all_gather(embed_table.astype(jnp.bfloat16), "dp", axis=0, tiled=True)
    rows_dev = embed_table.shape[0]
    slice_rows = vocab_slice.shape[0]
    gains_full = gain_rows.astype(jnp.float32)
    slot_len = token_ids.shape[1]
    model_width = w_out.shape[1]
    kv_width = KV_HEADS * HEAD_DIM
    ff_width = w_down.shape[0]
    group_size = HEADS // KV_HEADS
    row_count = 2 * COMP
    all_ids, all_marks, all_lengths, all_places = (
        lax.all_gather(token_ids, "shard", axis=0, tiled=True),
        lax.all_gather(completion_mask, "shard", axis=0, tiled=True),
        lax.all_gather(seq_lengths, "shard", axis=0, tiled=True),
        lax.all_gather(deal, "shard", axis=0, tiled=True),
    )
    group_seqs = all_places.shape[0]
    seq_numbers = jnp.arange(group_seqs, dtype=jnp.int32)
    place_hit = all_places[None, :] == seq_numbers[:, None]
    sources = jnp.sum(jnp.where(place_hit, seq_numbers[None, :], 0), axis=1).reshape(
        group_seqs // 2, 2
    )
    first_lens = jnp.take(all_lengths, sources[:, 0])
    step_ids = jnp.arange(slot_len, dtype=jnp.int32)
    index_rows = jnp.clip(slot_len - first_lens[:, None] + step_ids[None, :], 0, slot_len - 1)
    in_front = step_ids[None, :] < first_lens[:, None]

    def pack_one(table):
        front = jnp.take_along_axis(jnp.take(table, sources[:, 0], axis=0), index_rows, axis=1)
        back = jnp.take(table, sources[:, 1], axis=0)
        return jnp.where(in_front, front, back)

    packed_ids = pack_one(all_ids)
    packed_marks = pack_one(all_marks)
    chosen_all = jax.vmap(lambda marks: jnp.nonzero(marks, size=row_count)[0].astype(jnp.int32))(
        packed_marks
    )
    targets_all = jnp.take_along_axis(packed_ids, chosen_all + 1, axis=1)
    group_ids = packed_ids.reshape(-1)
    group_targets = targets_all.reshape(-1)
    chosen = chosen_all[shard_me]
    first_len = first_lens[shard_me]
    segment = (step_ids >= first_len).astype(jnp.int32)
    cos_rows, sin_rows = rotation((step_ids - segment * first_len).astype(jnp.float32))
    part_ids = group_ids
    owned_mask, local_row = locate(part_ids, rows_dev, shard_count, shard_me)
    looked_up = jnp.take(vocab_slice, local_row, axis=0).astype(jnp.float32)
    embedded = lax.psum_scatter(
        jnp.where(owned_mask[:, None], looked_up, 0.0).astype(jnp.bfloat16),
        "shard",
        scatter_dimension=0,
        tiled=True,
    ).astype(jnp.float32)
    normed_one = (embedded * rms_scale(embedded) * gains_full[0]).astype(jnp.bfloat16)
    mixed_rows = jnp.dot(normed_one, w_qkv, preferred_element_type=jnp.float32)
    queries = rotate(
        mixed_rows[:, :model_width].reshape(slot_len, HEADS, HEAD_DIM), cos_rows, sin_rows, 1.0
    ).astype(jnp.bfloat16)
    key_rows = rotate(
        mixed_rows[:, model_width : model_width + kv_width].reshape(slot_len, KV_HEADS, HEAD_DIM),
        cos_rows,
        sin_rows,
        1.0,
    ).astype(jnp.bfloat16)
    value_rows = (
        mixed_rows[:, model_width + kv_width :]
        .reshape(slot_len, KV_HEADS, HEAD_DIM)
        .astype(jnp.bfloat16)
    )
    key_wide = jnp.repeat(key_rows, group_size, axis=1)
    value_wide = jnp.repeat(value_rows, group_size, axis=1)
    block_len = min(512, slot_len)

    def block_scores(first_row):
        query_block = queries[first_row : first_row + block_len]
        raw_scores = (
            jnp.einsum("qhd,khd->hqk", query_block, key_wide, preferred_element_type=jnp.float32)
            * 0.125
        )
        rows_here = step_ids[first_row : first_row + block_len]
        segment_here = segment[first_row : first_row + block_len]
        allowed = (step_ids[None, :] <= rows_here[:, None]) & (
            segment[None, :] == segment_here[:, None]
        )
        return (query_block, jnp.where(allowed[None], raw_scores, masked_score))

    block_outputs = []
    lse_blocks = []
    for first_row in range(0, slot_len, block_len):
        _, scores = block_scores(first_row)
        row_top = jnp.max(scores, axis=-1, keepdims=True)
        exp_rows = jnp.exp(scores - row_top)
        row_total = jnp.sum(exp_rows, axis=-1, keepdims=True)
        prob_rows = (exp_rows / row_total).astype(jnp.bfloat16)
        block_outputs.append(
            jnp.einsum(
                "hqk,khd->qhd", prob_rows, value_wide, preferred_element_type=jnp.float32
            ).astype(jnp.bfloat16)
        )
        lse_blocks.append(row_top + jnp.log(row_total))
    attended = jnp.concatenate(block_outputs, axis=0).reshape(slot_len, model_width)
    resid_one = embedded + jnp.dot(attended, w_out, preferred_element_type=jnp.float32)
    normed_two = (resid_one * rms_scale(resid_one) * gains_full[1]).astype(jnp.bfloat16)
    gate_up = jnp.dot(normed_two, w_gate_up, preferred_element_type=jnp.float32)
    gate_part = gate_up[:, :ff_width]
    up_part = gate_up[:, ff_width:]
    hidden = (jax.nn.silu(gate_part) * up_part).astype(jnp.bfloat16)
    resid_two = resid_one + jnp.dot(hidden, w_down, preferred_element_type=jnp.float32)
    final_rows = (resid_two * rms_scale(resid_two) * gains_full[2]).astype(jnp.bfloat16)
    picked = jnp.take(final_rows, chosen, axis=0)
    group_rows = lax.all_gather(picked, "shard", axis=0, tiled=True)
    logits = contract_last(group_rows, vocab_slice)
    column_ids = jnp.arange(slice_rows, dtype=jnp.int32)
    target_owned, target_local = locate(group_targets, rows_dev, shard_count, shard_me)
    target_hot = (column_ids[None, :] == target_local[:, None]) & target_owned[:, None]
    top_logit = jnp.max(logits, axis=1)
    sum_exp = jnp.sum(jnp.exp(logits - top_logit[:, None]), axis=1)
    target_logit = jnp.sum(jnp.where(target_hot, logits, 0.0), axis=1)

    def combine(earlier, later):
        joint_top = jnp.maximum(earlier[0], later[0])
        joint_sum = earlier[1] * jnp.exp(earlier[0] - joint_top) + later[1] * jnp.exp(
            later[0] - joint_top
        )
        return (joint_top, joint_sum, earlier[2] + later[2])

    top_all, sum_all, target_all = merged((top_logit, sum_exp, target_logit), "shard", combine)
    lse_vocab = top_all + jnp.log(sum_all)
    row_losses = lse_vocab - target_all
    own_loss = jnp.sum(lax.dynamic_slice_in_dim(row_losses, shard_me * row_count, row_count, 0))
    packed_loss = jnp.mean(row_losses.reshape(group_seqs, COMP), axis=1)
    seq_loss = jnp.take(packed_loss, deal)
    d_logits = (
        (jnp.exp(logits - lse_vocab[:, None]) - target_hot.astype(jnp.float32)) / total_rows
    ).astype(jnp.bfloat16)
    d_slice_head = contract_first(d_logits, group_rows)
    d_picked = lax.psum_scatter(
        jnp.dot(
            lax.slice_in_dim(d_logits, 0, lax.axis_size("shard") * row_count, axis=0),
            vocab_slice,
            preferred_element_type=jnp.float32,
        ),
        "shard",
        scatter_dimension=0,
        tiled=True,
    )
    d_final = jnp.zeros((slot_len, model_width), jnp.float32).at[chosen].add(d_picked)
    d_resid_two, d_gain_three = norm_back(resid_two, gains_full[2], d_final)
    d_down = d_resid_two.astype(jnp.bfloat16)
    grad_down = contract_first(hidden, d_down)
    d_hidden = contract_last(d_down, w_down).astype(jnp.bfloat16).astype(jnp.float32)
    gate_sigmoid = jax.nn.sigmoid(gate_part)
    d_gate = d_hidden * up_part * gate_sigmoid * (1.0 + gate_part * (1.0 - gate_sigmoid))
    d_up = d_hidden * jax.nn.silu(gate_part)
    d_gate_up = jnp.concatenate([d_gate, d_up], axis=1).astype(jnp.bfloat16)
    grad_gate_up = contract_first(normed_two, d_gate_up)
    d_normed_two = contract_last(d_gate_up, w_gate_up)
    d_resid_norm, d_gain_two = norm_back(resid_one, gains_full[1], d_normed_two)
    d_resid_one = d_resid_two + d_resid_norm
    d_branch = d_resid_one.astype(jnp.bfloat16)
    grad_out = contract_first(attended, d_branch)
    d_attended = (
        contract_last(d_branch, w_out).astype(jnp.bfloat16).reshape(slot_len, HEADS, HEAD_DIM)
    )
    d_query_blocks = []
    d_key_wide = jnp.zeros((slot_len, HEADS, HEAD_DIM), jnp.float32)
    d_value_wide = jnp.zeros((slot_len, HEADS, HEAD_DIM), jnp.float32)
    for block_number, first_row in enumerate(range(0, slot_len, block_len)):
        query_block, scores = block_scores(first_row)
        prob_full = jnp.exp(scores - lse_blocks[block_number])
        d_out_block = d_attended[first_row : first_row + block_len]
        d_value_wide = d_value_wide + jnp.einsum(
            "hqk,qhd->khd",
            prob_full.astype(jnp.bfloat16),
            d_out_block,
            preferred_element_type=jnp.float32,
        )
        d_prob = jnp.einsum(
            "qhd,khd->hqk", d_out_block, value_wide, preferred_element_type=jnp.float32
        )
        d_scores = (
            prob_full * (d_prob - jnp.sum(d_prob * prob_full, axis=-1, keepdims=True))
        ).astype(jnp.bfloat16)
        d_query_blocks.append(
            jnp.einsum("hqk,khd->qhd", d_scores, key_wide, preferred_element_type=jnp.float32)
            * 0.125
        )
        d_key_wide = (
            d_key_wide
            + jnp.einsum("hqk,qhd->khd", d_scores, query_block, preferred_element_type=jnp.float32)
            * 0.125
        )
    d_queries = rotate(jnp.concatenate(d_query_blocks, axis=0), cos_rows, sin_rows, -1.0)
    d_keys = rotate(
        d_key_wide.reshape(slot_len, KV_HEADS, group_size, HEAD_DIM).sum(axis=2),
        cos_rows,
        sin_rows,
        -1.0,
    )
    d_values = d_value_wide.reshape(slot_len, KV_HEADS, group_size, HEAD_DIM).sum(axis=2)
    d_mixed = jnp.concatenate(
        [
            d_queries.reshape(slot_len, model_width),
            d_keys.reshape(slot_len, kv_width),
            d_values.reshape(slot_len, kv_width),
        ],
        axis=1,
    ).astype(jnp.bfloat16)
    grad_qkv = contract_first(normed_one, d_mixed)
    d_normed_one = contract_last(d_mixed, w_qkv)
    d_embed_norm, d_gain_one = norm_back(embedded, gains_full[0], d_normed_one)
    d_embedded = (d_resid_one + d_embed_norm).astype(jnp.bfloat16)
    part_ids = group_ids
    owned_mask, local_row = locate(part_ids, rows_dev, shard_count, shard_me)
    row_spots = jnp.where(owned_mask, local_row, slice_rows)
    d_slice = d_slice_head.at[row_spots].add(
        lax.all_gather(d_embedded, "shard", axis=0, tiled=True).astype(jnp.float32), mode="drop"
    )
    grad_table = lax.psum_scatter(d_slice, "dp", scatter_dimension=0, tiled=True)
    grad_gains = jnp.stack([d_gain_one, d_gain_two, d_gain_three], axis=0)
    full_grads = (grad_qkv, grad_out, grad_gate_up, grad_down, grad_gains)
    split_dims = (0, 0, 0, 0, 1)
    summed = lax.psum(
        (full_grads[0], full_grads[1], full_grads[2], full_grads[3], full_grads[4]), ("dp", "shard")
    )
    own_grads = tuple(
        (
            lax.dynamic_slice_in_dim(
                summed[number],
                shard_me * masters[number].shape[split_dims[number]],
                masters[number].shape[split_dims[number]],
                split_dims[number],
            )
            for number in range(5)
        )
    )
    layer_squares = sum((jnp.sum(gradient * gradient) for gradient in own_grads))
    layer_squares = jnp.where(lax.axis_index("dp") == 0, layer_squares, 0.0)
    table_squares = jnp.sum(grad_table * grad_table)
    loss_total, square_total = lax.psum((own_loss, layer_squares + table_squares), ("dp", "shard"))
    mean_loss = loss_total / total_rows
    grad_norm = jnp.sqrt(square_total)
    factor = max_norm / jnp.maximum(grad_norm, max_norm)
    firsts = (attend_in_first, attend_out_first, feed_in_first, feed_out_first, norm_gains_first)
    seconds = (
        attend_in_second,
        attend_out_second,
        feed_in_second,
        feed_out_second,
        norm_gains_second,
    )
    decays = (1.0, 1.0, 1.0, 1.0, 0.0)
    updated = [
        adamw_update(
            masters[number],
            firsts[number],
            seconds[number],
            own_grads[number] * factor,
            decays[number],
        )
        for number in range(5)
    ]
    table_new, table_first, table_second, _ = adamw_update(
        embed_table, embed_table_first, embed_table_second, grad_table * factor, 1.0
    )
    return (
        updated[0][0],
        updated[1][0],
        updated[2][0],
        updated[3][0],
        updated[4][3],
        table_new,
        updated[0][1],
        updated[1][1],
        updated[2][1],
        updated[3][1],
        updated[4][1],
        table_first,
        updated[0][2],
        updated[1][2],
        updated[2][2],
        updated[3][2],
        updated[4][2],
        table_second,
        mean_loss,
        grad_norm,
        seq_loss,
    )


def solution(mesh):
    in_specs = (
        P(("dp", "shard"), None),
        P(("dp", "shard")),
        P(("dp", "shard"), None),
        P(("dp", "shard")),
        P("shard", None),
        P("shard", None),
        P("shard", None),
        P("shard", None),
        P(None, "shard"),
        P(("dp", "shard"), None),
        P("shard", None),
        P("shard", None),
        P("shard", None),
        P("shard", None),
        P(None, "shard"),
        P(("dp", "shard"), None),
        P("shard", None),
        P("shard", None),
        P("shard", None),
        P("shard", None),
        P(None, "shard"),
        P(("dp", "shard"), None),
    )
    out_specs = (
        P("shard", None),
        P("shard", None),
        P("shard", None),
        P("shard", None),
        P(None, "shard"),
        P(("dp", "shard"), None),
        P("shard", None),
        P("shard", None),
        P("shard", None),
        P("shard", None),
        P(None, "shard"),
        P(("dp", "shard"), None),
        P("shard", None),
        P("shard", None),
        P("shard", None),
        P("shard", None),
        P(None, "shard"),
        P(("dp", "shard"), None),
        P(),
        P(),
        P(("dp", "shard")),
    )
    return jax.shard_map(
        per_device, mesh=mesh, in_specs=in_specs, out_specs=out_specs, check_vma=False
    )
```

profile of v0, /device:TPU:0, one launch (start us, length us, event | category | flops | bytes accessed | tf_op | source)
XLA Modules:
  0.0 2169.7 jit_solution(13546143062339284521)
XLA Ops:
  13.7 9.5 all-reduce.2
  33.5 8.9 all-gather.3
  44.8 50.4 %gather_fusion.9 = s32[8192]{0:T(1024)S(1)} fusion(s32[8,1024]{1,0:T(8,128)S(1)} %get-tuple-element.393, s32[8192]{0:T(1024)S(1)} %bitcast.191), kind=kCustom, calls=%fused_computation.5.clone | custom fusion | bytes 131072 | tf_op jit(solution)/shard_map/jit(take_along_axis)/gather | solution.py:163
  95.2 50.4 %gather_fusion.6 = s32[8192]{0:T(1024)S(1)} fusion(s32[8,1024]{1,0:T(8,128)S(1)} %get-tuple-element.394, s32[8192]{0:T(1024)S(1)} %bitcast.192), kind=kCustom, calls=%fused_computation.1.clone | custom fusion | bytes 131072 | tf_op jit(solution)/shard_map/jit(take_along_axis)/gather | solution.py:163
  147.2 73.0 %all-gather.16.cloned.1.call-done = bf16[6144,960]{0,1:T(8,128)(2,1)} async-done(((bf16[1536,960]{0,1:T(8,128)(2,1)}), bf16[6144,960]{0,1:T(8,128)(2,1)}) %all-gather.16.cloned.1.call-update) | async-done | bytes 11796496 | tf_op jit(solution)/shard_map/all_gather | solution.py:135
  220.2 16.3 copy.101
  236.5 46.9 %gather_fusion.1 = bf16[8192,960]{1,0:T(8,128)(2,1)} fusion(bf16[6144,960]{1,0:T(8,128)(2,1)} %copy.101, s32[8192]{0:T(1024)S(1)} %broadcast_clamp_fusion), kind=kCustom, calls=%fused_computation.7 | custom fusion | bytes 31490048 | tf_op jit(solution)/shard_map/jit(_take)/gather | solution.py:181
  283.4 20.6 copy.102
  304.1 14.6 select_convert_fusion
  331.2 56.7 %scatter_custom_fusion.2 = s32[256]{0:T(256)S(1)} fusion(s32[8192]{0:T(1024)S(1)} %bitcast.234, s32[8192]{0:T(1024)S(1)} %ne.299, s32[]{:T(128)} %constant.340.clone.1), kind=kCustom, calls=%fused_computation.306 | custom fusion | flops 8192 | bytes 1028
  388.9 9.2 all-gather.4
  405.0 19.4 reduce-scatter.4.cloned.1.call-done
  427.0 32.3 %all-gather.18.cloned.1.call-done = bf16[960,1600]{1,0:T(8,128)(2,1)} async-done(((bf16[120,1600]{1,0:T(8,128)(2,1)}), bf16[960,1600]{1,0:T(8,128)(2,1)}) %all-gather.18.cloned.1.call-update) | async-done | bytes 3072016 | tf_op jit(solution)/shard_map/all_gather | solution.py:129
  467.5 13.4 fusion.112
  480.9 13.5 fusion.113
  494.4 14.8 fusion.1
  509.4 13.0 fusion.44
  522.5 14.3 fusion
  536.8 12.6 fusion.43
  558.2 20.2 fusion.96
  578.4 10.9 multiply_convert_fusion.2
  594.9 9.4 multiply_reduce_fusion.7
  612.0 9.8 all_gather.64
  657.2 11.3 fusion.98
  668.6 36.0 %reduce-scatter.6.cloned.1.call-done = f32[32,960]{1,0:T(8,128)} async-done(((f32[256,960]{1,0:T(8,128)}), f32[32,960]{1,0:T(8,128)}) %reduce-scatter.6.cloned.1.call-update) | async-done | bytes 122896 | tf_op jit(solution)/shard_map/reduce_scatter | solution.py:271
  720.2 17.5 fusion.14
  737.7 19.0 multiply_reduce_fusion.4
  763.8 14.9 fusion.4
  778.7 24.0 %multiply_reduce_fusion = (f32[15,512]{1,0:T(8,128)S(1)}, f32[15,512,1024]{2,1,0:T(8,128)}) fusion(f32[15,512,1024]{2,1,0:T(8,128)} %get-tuple-element.396, f32[15,512]{1,0:T(8,128)S(1)} %log_add_fusion, bf16[512,15,64]{0,2,1:T(8,128)(2,1)S(1)} %bitcast.207, bf16[1024,15,64]{0,2,1:T(8,128)(2,1)S(1)} %bitcast.199), kind=kOutput, calls=%fused_computation.19 | convolution fusion | flops 1030218240 | bytes 65925120 | tf_op jit(solution)/shard_map/qhd,khd->hqk/dot_general | solution.py:312
  802.7 24.0 %multiply_reduce_fusion.1 = (f32[15,512]{1,0:T(8,128)S(1)}, f32[15,512,1024]{2,1,0:T(8,128)}) fusion(f32[15,512,1024]{2,1,0:T(8,128)} %get-tuple-element.398, f32[15,512]{1,0:T(8,128)S(1)} %log_add_fusion.1, bf16[512,15,64]{0,2,1:T(8,128)(2,1)S(1)} %bitcast.204, bf16[1024,15,64]{0,2,1:T(8,128)(2,1)S(1)} %bitcast.200), kind=kOutput, calls=%fused_computation.22 | convolution fusion | flops 1030218240 | bytes 65925120 | tf_op jit(solution)/shard_map/qhd,khd->hqk/dot_general | solution.py:312
  826.7 26.8 %multiply_convert_fusion.1 = bf16[15,512,1024]{2,1,0:T(8,128)(2,1)} fusion(f32[15,512,1024]{2,1,0:T(8,128)} %get-tuple-element.407, f32[15,512,1024]{2,1,0:T(8,128)} %get-tuple-element.398, f32[15,512]{1,0:T(8,128)S(1)} %get-tuple-element.406, f32[15,512]{1,0:T(8,128)S(1)} %log_add_fusion.1), kind=kLoop, calls=%fused_computation.21 | loop fusion | flops 31457280 | bytes 78704640 | tf_op jit(solution)/shard_map/convert_element_type | solution.py:317
  853.6 10.5 fusion.93
  864.1 11.6 multiply_bitcast_fusion.1
  875.7 16.3 fusion.37
  895.6 26.5 %multiply_convert_fusion = bf16[15,512,1024]{2,1,0:T(8,128)(2,1)} fusion(f32[15,512,1024]{2,1,0:T(8,128)} %get-tuple-element.409, f32[15,512,1024]{2,1,0:T(8,128)} %get-tuple-element.396, f32[15,512]{1,0:T(8,128)S(1)} %get-tuple-element.408, f32[15,512]{1,0:T(8,128)S(1)} %log_add_fusion), kind=kLoop, calls=%fused_computation.18 | loop fusion | flops 31457280 | bytes 78704640 | tf_op jit(solution)/shard_map/convert_element_type | solution.py:317
  922.1 11.6 multiply_bitcast_fusion
  933.7 11.7 add_multiply_fusion
  974.3 19.3 fusion.17
  993.6 10.9 fusion.115
  1005.6 15.9 fusion.97
  1021.4 24.5 %all-gather.26.cloned.1.call-done = bf16[8192,960]{0,1:T(8,128)(2,1)} async-done(((bf16[1024,960]{0,1:T(8,128)(2,1)}), bf16[8192,960]{0,1:T(8,128)(2,1)}) %all-gather.26.cloned.1.call-update) | async-done | bytes 15728656 | tf_op jit(solution)/shard_map/all_gather | solution.py:351
  1045.9 23.1 %copy.109 = f32[8192,960]{1,0:T(8,128)} copy(bf16[8192,960]{0,1:T(8,128)(2,1)} %all-gather.26.cloned.1.call-done) | data formatting | bytes 47185920 | tf_op jit(solution)/shard_map/convert_element_type | solution.py:351
  1069.0 89.5 %scatter_fusion = f32[6144,960]{1,0:T(8,128)} fusion(f32[6144,960]{1,0:T(8,128)} %fusion.97, s32[8192]{0:T(1024)S(1)} %bitcast.218, f32[8192,960]{1,0:T(8,128)} %copy.109), kind=kCustom, calls=%fused_computation.12 | custom fusion | flops 7864320 | bytes 94404608 | tf_op jit(solution)/shard_map/scatter-add | solution.py:350
  1179.8 41.1 %psum.53 = f32[3,960]{1,0:T(4,128)S(1)} all-reduce(f32[3,960]{1,0:T(4,128)S(1)} %pad_maximum_fusion.14), channel_id=1, replica_groups=mesh['dp'=4,'shard'=8] {'dp','shard'}, use_global_device_ids=true, to_apply=%region_38.41 | all-reduce | flops 2880 | bytes 23040 | tf_op jit(solution)/shard_map/psum | solution.py:357
  1221.6 420.1 %all-reduce.7.cloned.1.call-done = (f32[960,1600]{1,0:T(8,128)}, f32[960,960]{1,0:T(8,128)}, f32[960,5120]{1,0:T(8,128)}, f32[2560,960]{1,0:T(8,128)}) async-done(((f32[960,1600]{1,0:T(8,128)}, f32[960,960]{1,0:T(8,128)}, f32[960,5120]{1,0:T(8,128)}, f32[2560,960]{1,0:T(8,128)}), (f32[960,1600]{1,0:T(8,128)}, f32[960,960]{1,0:T(8,128)}, f32[960,5120]{1,0:T(8,128)}, ...) | async-done | bytes 39321616 | tf_op jit(solution)/shard_map/psum | solution.py:357
  1653.9 403.2 %reduce-scatter.8.cloned.1.call-done = f32[1536,960]{1,0:T(8,128)} async-done(((f32[6144,960]{1,0:T(8,128)}), f32[1536,960]{1,0:T(8,128)}) %reduce-scatter.8.cloned.1.call-update) | async-done | bytes 5898256 | tf_op jit(solution)/shard_map/reduce_scatter | solution.py:353
  2063.3 42.7 %all-reduce.3 = (f32[]{:T(128)}, f32[]{:T(128)}) all-reduce(f32[]{:T(128)S(6)} %add.700, f32[]{:T(128)} %dynamic-slice_reduce_fusion), channel_id=1, replica_groups=mesh['dp'=4,'shard'=8] {'dp','shard'}, use_global_device_ids=true, to_apply=%region_44.47 | all-reduce | flops 2 | bytes 16 | tf_op jit(solution)/shard_map/psum | solution.py:374
  2106.7 16.4 multiply_add_fusion.2
  (380 shorter events, 237.5 us)
Async XLA Ops:
  7.2 16.0 copy-start.60
  7.2 26.2 %copy-start.61 = (s32[2,1024]{1,0:T(2,128)S(1)}, s32[2,1024]{1,0:T(2,128)}, u32[]{:S(2)}) copy-start(s32[2,1024]{1,0:T(2,128)} %param.28) | copy-start | bytes 24580
  7.2 213.0 %all-gather.16.cloned.1.call-start = ((), (), s32[]{:S(2)}) async-start(), calls=%async_computation.3 | async-start | bytes 14745600 | tf_op jit(solution)/shard_map/all_gather | solution.py:135
  11.9 412.4 %reduce-scatter.4.cloned.1.call-start = ((), (), s32[]{:S(2)}) async-start(), calls=%async_computation.4 | async-start | bytes 17694720 | tf_op jit(solution)/shard_map/reduce_scatter | solution.py:182
  318.7 140.6 %all-gather.18.cloned.1.call-start = ((), (), s32[]{:S(2)}) async-start(), calls=%async_computation.5 | async-start | bytes 3594240 | tf_op jit(solution)/shard_map/all_gather | solution.py:129
  320.6 230.4 %all-gather.20.cloned.1.call-start = ((), (), s32[]{:S(2)}) async-start(), calls=%async_computation.6 | async-start | bytes 2211840 | tf_op jit(solution)/shard_map/all_gather | solution.py:130
  322.4 8.5 copy-start.70
  322.5 8.6 copy-start.69
  322.5 66.5 %copy-start.62 = (f32[3,120]{1,0:T(4,128)S(1)}, f32[3,120]{1,0:T(4,128)}, u32[]{:S(2)}) copy-start(f32[3,120]{1,0:T(4,128)} %param.36) | copy-start | bytes 4324
  322.5 235.7 %all-gather.22.cloned.1.call-start = ((), (), s32[]{:S(2)}) async-start(), calls=%async_computation.7 | async-start | bytes 11059200 | tf_op jit(solution)/shard_map/all_gather | solution.py:131
  323.7 271.2 %all-gather.24.cloned.1.call-start = ((), (), s32[]{:S(2)}) async-start(), calls=%async_computation.8 | async-start | bytes 5898240 | tf_op jit(solution)/shard_map/all_gather | solution.py:132
  326.1 378.5 %reduce-scatter.6.cloned.1.call-start = ((), (), s32[]{:S(2)}) async-start(), calls=%async_computation.9 | async-start | bytes 1179648 | tf_op jit(solution)/shard_map/reduce_scatter | solution.py:271
  388.2 38.1 %copy-start.72 = (s32[32]{0:T(128)}, s32[32]{0:T(128)S(1)}, u32[]{:S(2)}) copy-start(s32[32]{0:T(128)S(1)} %fusion.84) | copy-start | bytes 388
  398.8 67.0 %copy-start.52 = (f32[1,960]{1,0:T(1,128)}, f32[1,960]{1,0:T(1,128)S(1)}, u32[]{:S(2)}) copy-start(f32[1,960]{1,0:T(1,128)S(1)} %get-tuple-element.377) | copy-start | bytes 11524
  402.8 63.7 %copy-start.22 = (f32[1024,32]{0,1:T(8,128)}, f32[1024,32]{0,1:T(8,128)S(1)}, u32[]{:S(2)}) copy-start(f32[1024,32]{0,1:T(8,128)S(1)} %get-tuple-element.380) | copy-start | bytes 393220
  427.0 38.8 %copy-start.44 = (f32[1024]{0:T(1024)}, f32[1024]{0:T(1024)S(1)}, u32[]{:S(2)}) copy-start(f32[1024]{0:T(1024)S(1)} %get-tuple-element.382) | copy-start | bytes 12292
  467.2 13.7 copy-start.9
  467.2 13.7 copy-start.11
  467.5 13.4 copy-start
  509.4 27.4 %copy-start.6 = (bf16[1024,5,3,64]{0,3,2,1:T(8,128)(2,1)}, bf16[1024,5,3,64]{0,3,2,1:T(8,128)(2,1)S(1)}, u32[]{:S(2)}) copy-start(bf16[1024,5,3,64]{0,3,2,1:T(8,128)(2,1)S(1)} %broadcast_in_dim.189) | copy-start | bytes 5898244
  558.2 198.4 %copy-start.47 = (f32[1024]{0:T(1024)}, f32[1024]{0:T(1024)S(1)}, u32[]{:S(2)}) copy-start(f32[1024]{0:T(1024)S(1)} %get-tuple-element.384) | copy-start | bytes 12292
  589.3 17.0 copy-start.43
  621.8 6.7 copy-start.28
  621.8 14.7 copy-start.54
  621.8 14.7 copy-start.58
  628.5 8.0 copy-start.8
  657.2 11.3 copy-start.56
  668.5 377.4 %all-gather.26.cloned.1.call-start = ((), (), s32[]{:S(2)}) async-start(), calls=%async_computation.10 | async-start | bytes 17694720 | tf_op jit(solution)/shard_map/all_gather | solution.py:351
  720.2 17.5 copy-start.30
  737.7 19.0 copy-start.5
  763.8 38.9 %copy-start.15 = (bf16[512,960]{0,1:T(8,128)(2,1)}, bf16[512,960]{0,1:T(8,128)(2,1)S(1)}, u32[]{:S(2)}) copy-start(bf16[512,960]{0,1:T(8,128)(2,1)S(1)} %get-tuple-element.364) | copy-start | bytes 2949124
  763.8 14.9 copy-start.7
  826.7 26.9 %copy-start.10 = (bf16[1024,15,32]{0,2,1:T(8,128)(2,1)S(1)}, bf16[1024,15,32]{0,2,1:T(8,128)(2,1)}, u32[]{:S(2)}) copy-start(bf16[1024,15,32]{0,2,1:T(8,128)(2,1)} %copy-done.9) | copy-start | bytes 2949124
  826.7 26.9 %copy-start.12 = (bf16[1024,15,32]{0,2,1:T(8,128)(2,1)S(1)}, bf16[1024,15,32]{0,2,1:T(8,128)(2,1)}, u32[]{:S(2)}) copy-start(bf16[1024,15,32]{0,2,1:T(8,128)(2,1)} %copy-done.11) | copy-start | bytes 2949124
  853.6 10.5 copy-start.1
  960.5 681.3 %all-reduce.7.cloned.1.call-start = ((), (), s32[]{:S(2)}) async-start(), calls=%async_computation.12 | async-start | bytes 80936960 | tf_op jit(solution)/shard_map/psum | solution.py:357
  960.7 7.0 copy-start.34
  974.3 19.3 copy-start.31
  1004.6 1052.5 %reduce-scatter.8.cloned.1.call-start = ((), (), s32[]{:S(2)}) async-start(), calls=%async_computation.11 | async-start | bytes 31457280 | tf_op jit(solution)/shard_map/reduce_scatter | solution.py:353
  1021.4 47.6 %copy-start.42 = (s32[8192,1]{0,1:T(1,128)S(1)}, s32[8192,1]{0,1:T(1,128)}, u32[]{:S(2)}) copy-start(s32[8192,1]{0,1:T(1,128)} %get-tuple-element.345) | copy-start | bytes 98308
  1171.7 6.6 copy-start.77
  1171.7 6.6 copy-start.66
  1171.7 8.1 copy-start.49
  1171.7 8.1 copy-start.64
  1171.7 8.1 copy-start.65
  2135.9 6.6 copy-start.39
  2135.9 9.8 copy-start.32
  2135.9 9.8 copy-start.41
  (41 other events, 173.2 us)
Sparse Core Ops, SparseCore 0:
  12.1 208.1 all-gather.15
  318.8 105.5 reduce-scatter.3
  426.8 32.3 all-gather.17
  461.6 27.2 all-gather.19
  491.1 60.3 all-gather.21
  553.9 40.9 all-gather.23
  668.6 35.9 reduce-scatter.5
  960.6 85.2 all-gather.25
  1052.4 589.3 all-reduce.6
  1643.9 413.1 reduce-scatter.7
where the time goes:
time: 2180 us; the launch traced here: 2170 us
  waiting for transfers between devices  1010 us (46%)
  other arithmetic  360 us (17%)
  matrix products  341 us (16%)
  local copies, waits for them, and re-layouts  275 us (13%)
  blocking collectives  155 us (7%)
  between operations  24 us (1%)
    psum x1, waiting for transfers between devices, per_device(): lax.psum((full_grads[0], full_grads[1], full_grads[2], full_grads[3], ful...  420 us
    reduce_scatter x1, waiting for transfers between devices, per_device(): lax.psum_scatter(d_slice, 'dp', scatter_dimension=0, tiled=True)  403 us
    gather x4, local copies, waits for them, and re-layouts, pack_one(): jnp.take_along_axis(jnp.take(table, sources[:, 0], axis=0), index_rows, a...  101 us
    scatter-add x1, other arithmetic, per_device(): d_slice_head.at[row_spots]  89.5 us
    all_gather x1, waiting for transfers between devices, per_device(): lax.all_gather(embed_table.astype(jnp.bfloat16), 'dp', axis=0, tiled=True)  73 us
    gather x2, local copies, waits for them, and re-layouts, per_device(): looked_up = jnp.take(vocab_slice, local_row, axis=0).astype(jnp.float32)  67.5 us
    dot_general x5, matrix products, contract_first(): lax.dot_general(left, right, (((0,), (0,)), ((), ())), preferred_element_...  59.6 us
    unnamed x9, other arithmetic  57 us
  transfers between devices with their start and end apart: 10, of which 8 were waited for; matrix products, arithmetic and copies ran while one was open for 24% of the time, Pallas kernels for 0%

commit v1 on v0

--- a/solution.py
+++ b/solution.py
@@ -1,7 +1,15 @@
+import functools
+
 import jax
 import jax.numpy as jnp
+import numpy as np
 from jax import lax
+from jax.experimental import pallas as pl
+from jax.experimental.pallas import tpu as pltpu
 from jax.sharding import PartitionSpec as P
+
+MESH = pl.DeviceIdType.MESH
+VMEM = pltpu.MemorySpace.VMEM
 
 HEADS = 15
 KV_HEADS = 5
@@ -21,15 +29,250 @@
 masked_score = -1e30
 
 
-def merged(part, axis, combine):
-    gathered = jax.tree.map(lambda a: lax.all_gather(a, axis), part)
-
-    def take(source):
-        return jax.tree.map(lambda a: lax.dynamic_index_in_dim(a, source, 0, False), gathered)
-
-    return lax.fori_loop(
-        1, lax.axis_size(axis), lambda source, state: combine(state, take(source)), take(0)
-    )
+def bits_of(size):
+    return [1 << bit for bit in reversed(range(size.bit_length() - 1))]
+
+
+def place_of(dp_at, shard_at, dp_size, shard_size):
+    place, weight = 0, 1
+    for index, size in ((dp_at, dp_size), (shard_at, shard_size)):
+        for bit in bits_of(size):
+            place = place + (index // bit) % 2 * weight
+            weight *= 2
+    return place
+
+
+def exchange_stages(dp_size, shard_size):
+    return [(0, bit) for bit in bits_of(dp_size)] + [(1, bit) for bit in bits_of(shard_size)]
+
+
+def partner_of(me, axis, bit):
+    other = list(me)
+    other[axis] = me[axis] + bit - 2 * bit * ((me[axis] // bit) % 2)
+    return tuple(other)
+
+
+def here():
+    return (lax.axis_index("dp"), lax.axis_index("shard"))
+
+
+def greet_partners(me, stages):
+    barrier = pltpu.get_barrier_semaphore()
+    for axis, bit in stages:
+        pl.semaphore_signal(
+            barrier, inc=1, device_id=partner_of(me, axis, bit), device_id_type=MESH
+        )
+    pl.semaphore_wait(barrier, len(stages))
+
+
+def gather_kernel(sizes, x_ref, out_ref, send_sem, recv_sem, own_sem):
+    me = here()
+    stages = exchange_stages(*sizes)
+    place = place_of(*me, *sizes)
+    greet_partners(me, stages)
+    own = pltpu.make_async_copy(x_ref, out_ref.at[place], own_sem)
+    own.start()
+    own.wait()
+    for number, (axis, bit) in enumerate(stages):
+        span = 1 << number
+        start = place // span * span
+        copy = pltpu.make_async_remote_copy(
+            src_ref=out_ref.at[pl.ds(start, span)],
+            dst_ref=out_ref.at[pl.ds(start, span)],
+            send_sem=send_sem.at[number],
+            recv_sem=recv_sem.at[number],
+            device_id=partner_of(me, axis, bit),
+            device_id_type=MESH,
+        )
+        copy.start()
+        copy.wait()
+
+
+def gather_all(block, sizes, collective_id, name):
+    total = sizes[0] * sizes[1]
+    count = len(exchange_stages(*sizes))
+    return pl.pallas_call(
+        functools.partial(gather_kernel, sizes),
+        name=name,
+        out_shape=jax.ShapeDtypeStruct((total,) + block.shape, block.dtype),
+        in_specs=[pl.BlockSpec(memory_space=VMEM)],
+        out_specs=pl.BlockSpec(memory_space=VMEM),
+        scratch_shapes=[
+            pltpu.SemaphoreType.DMA((count,)),
+            pltpu.SemaphoreType.DMA((count,)),
+            pltpu.SemaphoreType.DMA,
+        ],
+        compiler_params=pltpu.CompilerParams(collective_id=collective_id, has_side_effects=True),
+    )(block)
+
+
+def scatter_kernel(sizes, x_ref, out_ref, total_ref, landed, send_sem, recv_sem):
+    me = here()
+    stages = exchange_stages(*sizes)
+    place = place_of(*me, *sizes)
+    greet_partners(me, stages)
+    base = 0
+    first = len(stages) - 1
+    for number in reversed(range(len(stages))):
+        axis, bit = stages[number]
+        span = 1 << number
+        mine = place // span * span
+        other = mine + span - 2 * span * ((mine // span) % 2)
+        parent = place // (2 * span) * (2 * span)
+        slot = landed.at[pl.ds(base, span)]
+        source = x_ref if number == first else total_ref
+        shift = 0 if number == first else parent
+        copy = pltpu.make_async_remote_copy(
+            src_ref=source.at[pl.ds(other - shift, span)],
+            dst_ref=slot,
+            send_sem=send_sem.at[number],
+            recv_sem=recv_sem.at[number],
+            device_id=partner_of(me, axis, bit),
+            device_id_type=MESH,
+        )
+        copy.start()
+        copy.wait()
+        kept = source[pl.ds(mine - shift, span)]
+        if number:
+            total_ref[pl.ds(0, span)] = kept + landed[base : base + span]
+        else:
+            out_ref[...] = (kept + landed[base : base + span])[0]
+        base += span
+
+
+def scatter_all(blocks, sizes, collective_id, name):
+    total = sizes[0] * sizes[1]
+    count = len(exchange_stages(*sizes))
+    return pl.pallas_call(
+        functools.partial(scatter_kernel, sizes),
+        name=name,
+        out_shape=jax.ShapeDtypeStruct(blocks.shape[1:], blocks.dtype),
+        in_specs=[pl.BlockSpec(memory_space=VMEM)],
+        out_specs=pl.BlockSpec(memory_space=VMEM),
+        scratch_shapes=[
+            pltpu.VMEM((total // 2,) + blocks.shape[1:], blocks.dtype),
+            pltpu.VMEM((total,) + blocks.shape[1:], blocks.dtype),
+            pltpu.SemaphoreType.DMA((count,)),
+            pltpu.SemaphoreType.DMA((count,)),
+        ],
+        compiler_params=pltpu.CompilerParams(collective_id=collective_id, has_side_effects=True),
+    )(blocks)
+
+
+def deal_kernel(
+    sizes, rows_ref, note_ref, out_ref, notes_ref, send_sem, recv_sem, note_send, note_recv, own_sem
+):
+    total = sizes[0] * sizes[1]
+    dp_at, shard_at = here()
+    me = dp_at * sizes[1] + shard_at
+    barrier = pltpu.get_barrier_semaphore()
+
+    def peer_at(step):
+        peer = lax.rem(me + step, total)
+        return peer, (peer // sizes[1], peer % sizes[1])
+
+    @pl.loop(1, total)
+    def _(step):
+        pl.semaphore_signal(barrier, inc=1, device_id=peer_at(step)[1], device_id_type=MESH)
+
+    own = pltpu.make_async_copy(rows_ref.at[me], out_ref.at[me], own_sem.at[0])
+    own.start()
+    own_note = pltpu.make_async_copy(note_ref, notes_ref.at[me], own_sem.at[1])
+    own_note.start()
+    pl.semaphore_wait(barrier, total - 1)
+
+    def copies(step):
+        peer, device = peer_at(step)
+        return (
+            pltpu.make_async_remote_copy(
+                src_ref=note_ref,
+                dst_ref=notes_ref.at[me],
+                send_sem=note_send.at[peer],
+                recv_sem=note_recv.at[me],
+                device_id=device,
+                device_id_type=MESH,
+            ),
+            pltpu.make_async_remote_copy(
+                src_ref=rows_ref.at[peer],
+                dst_ref=out_ref.at[me],
+                send_sem=send_sem.at[peer],
+                recv_sem=recv_sem.at[me],
+                device_id=device,
+                device_id_type=MESH,
+            ),
+        )
+
+    @pl.loop(1, total)
+    def _(step):
+        for copy in copies(step):
+            copy.start()
+
+    own.wait()
+    own_note.wait()
+
+    @pl.loop(1, total)
+    def _(step):
+        peer, device = peer_at(step)
+        for copy in copies(step):
+            copy.wait_send()
+        pltpu.make_async_remote_copy(
+            src_ref=note_ref,
+            dst_ref=notes_ref.at[peer],
+            send_sem=note_send.at[peer],
+            recv_sem=note_recv.at[peer],
+            device_id=device,
+            device_id_type=MESH,
+        ).wait_recv()
+        pltpu.make_async_remote_copy(
+            src_ref=rows_ref.at[peer],
+            dst_ref=out_ref.at[peer],
+            send_sem=send_sem.at[peer],
+            recv_sem=recv_sem.at[peer],
+            device_id=device,
+            device_id_type=MESH,
+        ).wait_recv()
+
+
+def deal_rows(rows, note, sizes, collective_id, name):
+    total = sizes[0] * sizes[1]
+    return pl.pallas_call(
+        functools.partial(deal_kernel, sizes),
+        name=name,
+        out_shape=(
+            jax.ShapeDtypeStruct(rows.shape, rows.dtype),
+            jax.ShapeDtypeStruct((total,) + note.shape, note.dtype),
+        ),
+        in_specs=[pl.BlockSpec(memory_space=VMEM)] * 2,
+        out_specs=(pl.BlockSpec(memory_space=VMEM),) * 2,
+        scratch_shapes=[pltpu.SemaphoreType.DMA((total,))] * 4 + [pltpu.SemaphoreType.DMA((2,))],
+        compiler_params=pltpu.CompilerParams(collective_id=collective_id, has_side_effects=True),
+    )(rows, note)
+
+
+def count_kernel(high_count, high_ref, low_ref, out_ref):
+    high_pad = out_ref.shape[1]
+
+    @pl.loop(0, high_ref.shape[0])
+    def _(n):
+        length = high_ref.shape[2]
+        high_hot = (
+            lax.broadcasted_iota(jnp.int32, (high_pad, length), 0) == high_ref[n]
+        ).astype(jnp.float32)
+        low_hot = (lax.broadcasted_iota(jnp.int32, (128, length), 0) == low_ref[n]).astype(
+            jnp.float32
+        )
+        out_ref[n] = contract_last(high_hot.astype(jnp.bfloat16), low_hot.astype(jnp.bfloat16))
+
+
+def count_rows(high, low, high_pad):
+    count, length = high.shape
+    return pl.pallas_call(
+        functools.partial(count_kernel, high_pad),
+        name="count_rows",
+        out_shape=jax.ShapeDtypeStruct((count, high_pad, 128), jnp.float32),
+        in_specs=[pl.BlockSpec(memory_space=VMEM)] * 2,
+        out_specs=pl.BlockSpec(memory_space=VMEM),
+    )(high.reshape(count, 1, length), low.reshape(count, 1, length))
 
 
 def contract_last(left, right):
@@ -75,13 +318,6 @@
         ],
         axis=-1,
     )
-
-
-def locate(id_rows, rows_dev, shard_count, shard_me):
-    block_id = id_rows // rows_dev
-    owned_mask = block_id % shard_count == shard_me
-    local_row = block_id // shard_count * rows_dev + id_rows % rows_dev
-    return (owned_mask, local_row)
 
 
 def adamw_update(master, first_old, second_old, gradient, decay_on):
@@ -121,8 +357,14 @@
 ):
     shard_count = lax.axis_size("shard")
     group_count = lax.axis_size("dp")
-    shard_me = lax.axis_index("shard")
-    total_rows = 2 * COMP * shard_count * group_count
+    sizes = (group_count, shard_count)
+    device_count = shard_count * group_count
+    dp_me, shard_me = here()
+    device_me = dp_me * shard_count + shard_me
+    place_me = place_of(dp_me, shard_me, *sizes)
+    total_rows = 2 * COMP * device_count
+    slot_len = token_ids.shape[1]
+    model_width = attend_out.shape[1]
     masters = (attend_in, attend_out, feed_in, feed_out, norm_gains)
     copies = tuple((master.astype(jnp.bfloat16) for master in masters))
     w_qkv, w_out, w_gate_up, w_down, gain_rows = (
@@ -132,59 +374,149 @@
         lax.all_gather(copies[3], "shard", axis=0, tiled=True),
         lax.all_gather(copies[4], "shard", axis=1, tiled=True),
     )
-    vocab_slice = lax.all_gather(embed_table.astype(jnp.bfloat16), "dp", axis=0, tiled=True)
+    table_rows = embed_table.astype(jnp.bfloat16)
     rows_dev = embed_table.shape[0]
-    slice_rows = vocab_slice.shape[0]
     gains_full = gain_rows.astype(jnp.float32)
-    slot_len = token_ids.shape[1]
-    model_width = w_out.shape[1]
     kv_width = KV_HEADS * HEAD_DIM
     ff_width = w_down.shape[0]
     group_size = HEADS // KV_HEADS
     row_count = 2 * COMP
-    all_ids, all_marks, all_lengths, all_places = (
-        lax.all_gather(token_ids, "shard", axis=0, tiled=True),
-        lax.all_gather(completion_mask, "shard", axis=0, tiled=True),
-        lax.all_gather(seq_lengths, "shard", axis=0, tiled=True),
-        lax.all_gather(deal, "shard", axis=0, tiled=True),
-    )
-    group_seqs = all_places.shape[0]
-    seq_numbers = jnp.arange(group_seqs, dtype=jnp.int32)
-    place_hit = all_places[None, :] == seq_numbers[:, None]
-    sources = jnp.sum(jnp.where(place_hit, seq_numbers[None, :], 0), axis=1).reshape(
-        group_seqs // 2, 2
-    )
-    first_lens = jnp.take(all_lengths, sources[:, 0])
+
+    side = jnp.concatenate(
+        [
+            seq_lengths[:, None],
+            deal[:, None],
+            jnp.zeros((token_ids.shape[0], 126), jnp.int32),
+        ],
+        axis=1,
+    )
+    seqs_all = gather_all(
+        jnp.concatenate([token_ids * 2 + completion_mask, side], axis=1), sizes, 1, "gather_ids"
+    )
+    seqs_all = seqs_all.reshape(-1, slot_len + 128)
+    lengths_all = seqs_all[:, slot_len]
+    places_all = seqs_all[:, slot_len + 1]
+    order = sorted(
+        ((dp_at, shard_at) for dp_at in range(group_count) for shard_at in range(shard_count)),
+        key=lambda at: place_of(*at, *sizes),
+    )
+    seqs_dev = token_ids.shape[0]
+    group_of = jnp.asarray(np.repeat([at[0] for at in order], seqs_dev).astype(np.int32))
+    buffer_of = group_of * shard_count + places_all // 2
     step_ids = jnp.arange(slot_len, dtype=jnp.int32)
-    index_rows = jnp.clip(slot_len - first_lens[:, None] + step_ids[None, :], 0, slot_len - 1)
-    in_front = step_ids[None, :] < first_lens[:, None]
-
-    def pack_one(table):
-        front = jnp.take_along_axis(jnp.take(table, sources[:, 0], axis=0), index_rows, axis=1)
-        back = jnp.take(table, sources[:, 1], axis=0)
-        return jnp.where(in_front, front, back)
-
-    packed_ids = pack_one(all_ids)
-    packed_marks = pack_one(all_marks)
-    chosen_all = jax.vmap(lambda marks: jnp.nonzero(marks, size=row_count)[0].astype(jnp.int32))(
-        packed_marks
-    )
-    targets_all = jnp.take_along_axis(packed_ids, chosen_all + 1, axis=1)
-    group_ids = packed_ids.reshape(-1)
-    group_targets = targets_all.reshape(-1)
-    chosen = chosen_all[shard_me]
-    first_len = first_lens[shard_me]
+
+    def own_row(half):
+        hit = (group_of == dp_me) & (places_all == 2 * shard_me + half)
+        return jnp.sum(jnp.where(hit[:, None], seqs_all, 0), axis=0)
+
+    front_row, back_row = own_row(0), own_row(1)
+    first_len = front_row[slot_len]
+    front_slot = front_row[:slot_len]
+    packed = jnp.where(
+        step_ids < first_len,
+        lax.dynamic_slice_in_dim(
+            jnp.concatenate([front_slot, front_slot]), slot_len - first_len, slot_len
+        ),
+        back_row[:slot_len],
+    )
+    own_ids = packed // 2
+    own_marks = packed % 2
+    marks_before = jnp.sum(
+        jnp.where(step_ids[None, :] <= step_ids[:, None], own_marks[None, :], 0), axis=1
+    )
+    chosen_hot = (
+        marks_before[None, :] == 1 + jnp.arange(row_count, dtype=jnp.int32)[:, None]
+    ) & (own_marks[None, :] == 1)
+    own_targets = jnp.sum(jnp.where(chosen_hot, jnp.roll(own_ids, -1)[None, :], 0), axis=1)
     segment = (step_ids >= first_len).astype(jnp.int32)
     cos_rows, sin_rows = rotation((step_ids - segment * first_len).astype(jnp.float32))
-    part_ids = group_ids
-    owned_mask, local_row = locate(part_ids, rows_dev, shard_count, shard_me)
-    looked_up = jnp.take(vocab_slice, local_row, axis=0).astype(jnp.float32)
-    embedded = lax.psum_scatter(
-        jnp.where(owned_mask[:, None], looked_up, 0.0).astype(jnp.bfloat16),
-        "shard",
-        scatter_dimension=0,
-        tiled=True,
+
+    deal_cap = -(-3 * slot_len // (2 * device_count) // 16) * 16
+    ids_all = seqs_all[:, :slot_len] // 2
+    near = ids_all - device_me * rows_dev
+    wanted = (
+        (near >= 0)
+        & (near < rows_dev)
+        & (step_ids[None, :] >= slot_len - lengths_all[:, None])
+    )
+    high_count = -(-rows_dev // 128)
+    high_pad = -(-high_count // 8) * 8
+    seen = count_rows(
+        jnp.where(wanted, near // 128, -1), jnp.where(wanted, near % 128, -1), high_pad
+    )[:, :high_count]
+    buffer_hot = (
+        buffer_of[None, :] == jnp.arange(device_count, dtype=jnp.int32)[:, None]
     ).astype(jnp.float32)
+    seen_by = (
+        jnp.einsum("bn,nhl->bhl", buffer_hot, jnp.minimum(seen, 1.0)) > 0.5
+    ).astype(jnp.float32)
+    upto = (jnp.arange(128)[:, None] <= jnp.arange(128)[None, :]).astype(jnp.float32)
+    within = jnp.einsum("bhl,lm->bhm", seen_by, upto)
+    whole = within[:, :, -1]
+    before = (jnp.arange(high_count)[:, None] < jnp.arange(high_count)[None, :]).astype(jnp.float32)
+    rank_by = within + jnp.einsum("bh,hg->bg", whole, before)[:, :, None]
+    rank_by = jnp.where(seen_by > 0.5, rank_by, 0.0).reshape(device_count, -1)[:, :rows_dev]
+
+    owner = own_ids // rows_dev
+    same_id = own_ids[None, :] == own_ids[:, None]
+    is_first = (
+        jnp.sum(jnp.where(same_id & (step_ids[None, :] < step_ids[:, None]), 1, 0), axis=1) == 0
+    )
+    rank_own = jnp.sum(
+        jnp.where(
+            is_first[None, :]
+            & (owner[None, :] == owner[:, None])
+            & (own_ids[None, :] < own_ids[:, None]),
+            1,
+            0,
+        ),
+        axis=1,
+    )
+    rounds_own = jnp.max(rank_own) // deal_cap + 1
+
+    def send_hot(turn):
+        spots = (turn * deal_cap + 1 + jnp.arange(deal_cap, dtype=jnp.int32)).astype(jnp.float32)
+        return (
+            (rank_by[:, None, :] == spots[None, :, None])
+            .astype(jnp.bfloat16)
+            .reshape(device_count * deal_cap, rows_dev)
+        )
+
+    def take_hot(turn):
+        slot = rank_own - turn * deal_cap
+        inside = (slot >= 0) & (slot < deal_cap)
+        spot = jnp.where(inside, owner * deal_cap + slot, -1)
+        return (
+            spot[:, None] == jnp.arange(device_count * deal_cap, dtype=jnp.int32)[None, :]
+        ).astype(jnp.bfloat16)
+
+    def fetch(turn, note):
+        rows_out = jnp.dot(send_hot(turn), table_rows, preferred_element_type=jnp.float32)
+        landed, notes = deal_rows(
+            rows_out.astype(jnp.bfloat16).reshape(device_count, deal_cap, model_width),
+            note,
+            sizes,
+            2,
+            "deal_rows",
+        )
+        found = jnp.dot(
+            take_hot(turn),
+            landed.reshape(device_count * deal_cap, model_width),
+            preferred_element_type=jnp.float32,
+        )
+        return found, notes
+
+    note_shape = (-(-3 * model_width // 1024) * 8, 128)
+    embedded, round_notes = fetch(
+        0, jnp.broadcast_to(rounds_own.astype(jnp.float32), note_shape)
+    )
+    rounds = jnp.max(round_notes[:, 0, 0]).astype(jnp.int32)
+    embedded = lax.fori_loop(
+        1,
+        rounds,
+        lambda turn, held: held + fetch(turn, jnp.zeros(note_shape, jnp.float32))[0],
+        embedded,
+    )
     normed_one = (embedded * rms_scale(embedded) * gains_full[0]).astype(jnp.bfloat16)
     mixed_rows = jnp.dot(normed_one, w_qkv, preferred_element_type=jnp.float32)
     queries = rotate(
@@ -241,44 +573,70 @@
     hidden = (jax.nn.silu(gate_part) * up_part).astype(jnp.bfloat16)
     resid_two = resid_one + jnp.dot(hidden, w_down, preferred_element_type=jnp.float32)
     final_rows = (resid_two * rms_scale(resid_two) * gains_full[2]).astype(jnp.bfloat16)
-    picked = jnp.take(final_rows, chosen, axis=0)
-    group_rows = lax.all_gather(picked, "shard", axis=0, tiled=True)
-    logits = contract_last(group_rows, vocab_slice)
-    column_ids = jnp.arange(slice_rows, dtype=jnp.int32)
-    target_owned, target_local = locate(group_targets, rows_dev, shard_count, shard_me)
-    target_hot = (column_ids[None, :] == target_local[:, None]) & target_owned[:, None]
+    chosen_rows = chosen_hot.astype(jnp.bfloat16)
+    picked = jnp.dot(chosen_rows, final_rows, preferred_element_type=jnp.float32)
+    pad_width = -(-(model_width + 2) // 128) * 128 - model_width - 2
+    tagged = jnp.concatenate(
+        [
+            picked,
+            (own_targets // 256).astype(jnp.float32)[:, None],
+            (own_targets % 256).astype(jnp.float32)[:, None],
+            jnp.zeros((row_count, pad_width), jnp.float32),
+        ],
+        axis=1,
+    ).astype(jnp.bfloat16)
+    tagged_all = gather_all(tagged, sizes, 3, "gather_rows").reshape(total_rows, -1)
+    rows_all = tagged_all[:, :model_width]
+    targets_all = tagged_all[:, model_width].astype(jnp.int32) * 256 + tagged_all[
+        :, model_width + 1
+    ].astype(jnp.int32)
+    logits = contract_last(rows_all, table_rows)
+    target_hot = (targets_all - device_me * rows_dev)[:, None] == jnp.arange(
+        rows_dev, dtype=jnp.int32
+    )[None, :]
     top_logit = jnp.max(logits, axis=1)
     sum_exp = jnp.sum(jnp.exp(logits - top_logit[:, None]), axis=1)
     target_logit = jnp.sum(jnp.where(target_hot, logits, 0.0), axis=1)
-
-    def combine(earlier, later):
-        joint_top = jnp.maximum(earlier[0], later[0])
-        joint_sum = earlier[1] * jnp.exp(earlier[0] - joint_top) + later[1] * jnp.exp(
-            later[0] - joint_top
-        )
-        return (joint_top, joint_sum, earlier[2] + later[2])
-
-    top_all, sum_all, target_all = merged((top_logit, sum_exp, target_logit), "shard", combine)
+    stats = gather_all(
+        jnp.concatenate([top_logit, sum_exp, target_logit]).reshape(3 * total_rows // 128, 128),
+        sizes,
+        4,
+        "gather_stats",
+    ).reshape(device_count, 3, total_rows)
+    top_all = jnp.max(stats[:, 0], axis=0)
+    sum_all = jnp.sum(stats[:, 1] * jnp.exp(stats[:, 0] - top_all[None, :]), axis=0)
     lse_vocab = top_all + jnp.log(sum_all)
-    row_losses = lse_vocab - target_all
-    own_loss = jnp.sum(lax.dynamic_slice_in_dim(row_losses, shard_me * row_count, row_count, 0))
-    packed_loss = jnp.mean(row_losses.reshape(group_seqs, COMP), axis=1)
-    seq_loss = jnp.take(packed_loss, deal)
+    row_losses = lse_vocab - jnp.sum(stats[:, 2], axis=0)
+    mean_loss = jnp.sum(row_losses) / total_rows
+    packed_loss = jnp.mean(row_losses.reshape(-1, COMP), axis=1)
+    loss_at = place_of(dp_me, deal // 2, *sizes) * 2 + deal % 2
+    seq_loss = jnp.sum(
+        jnp.where(
+            loss_at[:, None] == jnp.arange(packed_loss.shape[0], dtype=jnp.int32)[None, :],
+            packed_loss[None, :],
+            0.0,
+        ),
+        axis=1,
+    )
     d_logits = (
         (jnp.exp(logits - lse_vocab[:, None]) - target_hot.astype(jnp.float32)) / total_rows
     ).astype(jnp.bfloat16)
-    d_slice_head = contract_first(d_logits, group_rows)
-    d_picked = lax.psum_scatter(
-        jnp.dot(
-            lax.slice_in_dim(d_logits, 0, lax.axis_size("shard") * row_count, axis=0),
-            vocab_slice,
-            preferred_element_type=jnp.float32,
+    d_table_head = contract_first(d_logits, rows_all)
+    d_picked = scatter_all(
+        jnp.dot(d_logits, table_rows, preferred_element_type=jnp.float32).reshape(
+            device_count, row_count, model_width
         ),
-        "shard",
-        scatter_dimension=0,
-        tiled=True,
-    )
-    d_final = jnp.zeros((slot_len, model_width), jnp.float32).at[chosen].add(d_picked)
+        sizes,
+        5,
+        "scatter_rows",
+    )
+    d_final = lax.dot_general(
+        chosen_hot.astype(jnp.float32),
+        d_picked,
+        (((0,), (0,)), ((), ())),
+        precision=lax.Precision.HIGHEST,
+        preferred_element_type=jnp.float32,
+    )
     d_resid_two, d_gain_three = norm_back(resid_two, gains_full[2], d_final)
     d_down = d_resid_two.astype(jnp.bfloat16)
     grad_down = contract_first(hidden, d_down)
@@ -344,36 +702,51 @@
     d_normed_one = contract_last(d_mixed, w_qkv)
     d_embed_norm, d_gain_one = norm_back(embedded, gains_full[0], d_normed_one)
     d_embedded = (d_resid_one + d_embed_norm).astype(jnp.bfloat16)
-    part_ids = group_ids
-    owned_mask, local_row = locate(part_ids, rows_dev, shard_count, shard_me)
-    row_spots = jnp.where(owned_mask, local_row, slice_rows)
-    d_slice = d_slice_head.at[row_spots].add(
-        lax.all_gather(d_embedded, "shard", axis=0, tiled=True).astype(jnp.float32), mode="drop"
-    )
-    grad_table = lax.psum_scatter(d_slice, "dp", scatter_dimension=0, tiled=True)
     grad_gains = jnp.stack([d_gain_one, d_gain_two, d_gain_three], axis=0)
-    full_grads = (grad_qkv, grad_out, grad_gate_up, grad_down, grad_gains)
-    split_dims = (0, 0, 0, 0, 1)
-    summed = lax.psum(
-        (full_grads[0], full_grads[1], full_grads[2], full_grads[3], full_grads[4]), ("dp", "shard")
-    )
+    gain_note = jnp.pad(
+        grad_gains.reshape(-1), (0, note_shape[0] * 128 - 3 * model_width)
+    ).reshape(note_shape)
+
+    def give(turn):
+        rows_out = contract_first(take_hot(turn), d_embedded)
+        landed, notes = deal_rows(
+            rows_out.astype(jnp.bfloat16).reshape(device_count, deal_cap, model_width),
+            gain_note,
+            sizes,
+            2,
+            "deal_rows",
+        )
+        return (
+            contract_first(
+                send_hot(turn), landed.reshape(device_count * deal_cap, model_width)
+            ),
+            notes,
+        )
+
+    d_table_tokens, gain_notes = give(0)
+    grad_table = lax.fori_loop(
+        1, rounds, lambda turn, held: held + give(turn)[0], d_table_head + d_table_tokens
+    )
+    gain_total = (
+        jnp.sum(gain_notes, axis=0).reshape(-1)[: 3 * model_width].reshape(3, model_width)
+    )
+    gain_width = norm_gains.shape[1]
     own_grads = tuple(
-        (
-            lax.dynamic_slice_in_dim(
-                summed[number],
-                shard_me * masters[number].shape[split_dims[number]],
-                masters[number].shape[split_dims[number]],
-                split_dims[number],
-            )
-            for number in range(5)
-        )
-    )
+        lax.psum(
+            lax.psum_scatter(
+                gradient.astype(jnp.bfloat16), "shard", scatter_dimension=0, tiled=True
+            ),
+            "dp",
+        ).astype(jnp.float32)
+        for gradient in (grad_qkv, grad_out, grad_gate_up, grad_down)
+    ) + (lax.dynamic_slice_in_dim(gain_total, shard_me * gain_width, gain_width, 1),)
     layer_squares = sum((jnp.sum(gradient * gradient) for gradient in own_grads))
-    layer_squares = jnp.where(lax.axis_index("dp") == 0, layer_squares, 0.0)
+    layer_squares = jnp.where(dp_me == 0, layer_squares, 0.0)
     table_squares = jnp.sum(grad_table * grad_table)
-    loss_total, square_total = lax.psum((own_loss, layer_squares + table_squares), ("dp", "shard"))
-    mean_loss = loss_total / total_rows
-    grad_norm = jnp.sqrt(square_total)
+    squares_all = gather_all(
+        jnp.broadcast_to(layer_squares + table_squares, (8, 128)), sizes, 6, "gather_squares"
+    )
+    grad_norm = jnp.sqrt(jnp.sum(squares_all[:, 0, 0]))
     factor = max_norm / jnp.maximum(grad_norm, max_norm)
     firsts = (attend_in_first, attend_out_first, feed_in_first, feed_out_first, norm_gains_first)
     seconds = (

time: 2180 us -> 1160 us (0.53)
  waiting for transfers between devices: 1010 us -> 180 us
  Pallas kernels: 0 us -> 337 us
  local copies, waits for them, and re-layouts: 275 us -> 46.2 us
  other arithmetic: 360 us -> 194 us
  blocking collectives: 155 us -> 9.32 us
  matrix products: 341 us -> 364 us
    reduce_scatter x3, waiting for transfers between devices: 459 us -> 84.5 us  [per_device(): lax.psum_scatter(gradient.astype(jnp.bfloat16), 'shard', scatter_dimensio...]
    pallas_call x0 -> x8, Pallas kernels: none -> 337 us  [the longest x2 155 us: deal_rows(): pl.pallas_call(functools.partial(deal_kernel, sizes), name=name, out_shap...]
    psum x1, waiting for transfers between devices: 420 us -> 95.2 us  [per_device(): lax.psum(lax.psum_scatter(gradient.astype(jnp.bfloat16), 'shard', scatter...]
    gather x16 -> x0, local copies, waits for them, and re-layouts: 177 us -> none  [the longest x4 101 us: pack_one(): jnp.take_along_axis(jnp.take(table, sources[:, 0], axis=0), index_rows, a...]
    all_gather x2 -> x0, waiting for transfers between devices: 97.5 us -> none  [the longest x1 73 us: per_device(): lax.all_gather(embed_table.astype(jnp.bfloat16), 'dp', axis=0, tiled=True)]
    scatter-add x2 -> x0, other arithmetic: 93 us -> none  [the longest x1 89.5 us: per_device(): d_slice_head.at[row_spots]]
    psum x2 -> x0, blocking collectives: 83.8 us -> none  [the longest x1 42.7 us: per_device(): lax.psum((own_loss, layer_squares + table_squares), ('dp', 'shard'))]
    unnamed x9 -> x3, other arithmetic: 57 us -> 0.01 us
  transfers between devices with their start and end apart: 10 -> 9, of which waited for: 8 -> 2; matrix products, arithmetic and copies ran while one was open for 24% -> 36% of each run, Pallas kernels for 0% -> 16%
where the time goes in v1:
time: 1160 us
  matrix products  364 us (31%)
  Pallas kernels  337 us (29%)
  other arithmetic  194 us (17%)
  waiting for transfers between devices  180 us (16%)
  local copies, waits for them, and re-layouts  46.2 us (4%)
  between operations  27 us (2%)
    pallas_call x2, Pallas kernels, deal_rows(): pl.pallas_call(functools.partial(deal_kernel, sizes), name=name, out_shap...  155 us
    pallas_call x4, Pallas kernels, gather_all(): pl.pallas_call(functools.partial(gather_kernel, sizes), name=name, out_sh...  105 us
    psum x1, waiting for transfers between devices, per_device(): lax.psum(lax.psum_scatter(gradient.astype(jnp.bfloat16), 'shard', scatter...  95.2 us
    reduce_scatter x3, waiting for transfers between devices, per_device(): lax.psum_scatter(gradient.astype(jnp.bfloat16), 'shard', scatter_dimensio...  84.5 us
    pallas_call x1, Pallas kernels, scatter_all(): pl.pallas_call(functools.partial(scatter_kernel, sizes), name=name, out_s...  61.2 us
    dot_general x7, matrix products, contract_first(): lax.dot_general(left, right, (((0,), (0,)), ((), ())), preferred_element_...  58 us
    dot_general x5, matrix products, contract_last(): lax.dot_general(left, right, (((1,), (1,)), ((), ())), preferred_element_...  56.6 us
    convert_element_type x2, other arithmetic, per_device(): d_scores = (prob_full * (d_prob - jnp.sum(d_prob * prob_full, axis=-1, ke...  52.9 us
  transfers between devices with their start and end apart: 9, of which 2 were waited for; matrix products, arithmetic and copies ran while one was open for 36% of the time, Pallas kernels for 16%

profile of v1, /device:TPU:0, one launch (start us, length us, event | category | flops | bytes accessed | tf_op | source)
XLA Modules:
  0.0 1158.3 jit_solution(14336857851214190003)
XLA Ops:
  15.8 19.6 %gather_ids.1 = s32[32,2,1152]{2,1,0:T(2,128)} custom-call(s32[2,1152]{1,0:T(2,128)} %concatenate.54.x_ref), custom_call_target="tpu_custom_call" | custom-call | tf_op jit(solution)/shard_map/gather_ids/pallas_call | solution.py:94
  50.0 15.4 %count_rows.1 = f32[64,16,128]{2,1,0:T(8,128)} custom-call(s32[64,1,1024]{2,1,0:T(1,128)} %copy.132.high_ref, s32[64,1,1024]{2,1,0:T(1,128)} %reshape.545.low_ref), custom_call_target="tpu_custom_call" | custom-call | tf_op jit(solution)/shard_map/count_rows/pallas_call | solution.py:269
  67.6 9.3 all-gather
  79.5 5.3 copy.136
  86.2 7.2 convolution_convert_fusion.5
  96.9 77.5 %deal_rows.4 = (bf16[32,48,960]{2,1,0:T(8,128)(2,1)}, f32[32,24,128]{2,1,0:T(8,128)}) custom-call(bf16[32,48,960]{2,1,0:T(8,128)(2,1)} %bitcast.193, f32[24,128]{1,0:T(8,128)} %broadcast_in_dim.143.note_ref), custom_call_target="tpu_custom_call" | custom-call | tf_op jit(solution)/shard_map/deal_rows/pallas_call | solution.py:238
  176.7 7.3 fusion.33
  193.8 7.1 fusion.136
  205.7 13.3 %fusion.151 = (f32[15,512]{1,0:T(8,128)S(1)}, f32[15,512,1024]{2,1,0:T(8,128)}) fusion(bf16[1024,15,64]{0,2,1:T(8,128)(2,1)S(1)} %bitcast.175, bf16[1024,15,32]{0,2,1:T(8,128)(2,1)S(1)} %get-tuple-element.268, bf16[1024,15,32]{0,2,1:T(8,128)(2,1)S(1)} %get-tuple-element.267, pred[512,1024]{1,0:T(8,128)(4,1)S(1)} %get-tuple-element.296), kind=kOutput, calls=%fused_computation.358 | convolution fusion | flops 1032184320 | bytes 35944448 | tf_op jit(solution)/shard_map/qhd,khd->hqk/dot_general | solution.py:543
  219.0 13.1 %fusion.152 = (f32[15,512]{1,0:T(8,128)S(1)}, f32[15,512,1024]{2,1,0:T(8,128)}) fusion(bf16[1024,15,64]{0,2,1:T(8,128)(2,1)S(1)} %bitcast.176, bf16[1024,15,32]{0,2,1:T(8,128)(2,1)S(1)} %get-tuple-element.267, bf16[1024,15,32]{0,2,1:T(8,128)(2,1)S(1)} %get-tuple-element.268, pred[512,1024]{1,0:T(8,128)(4,1)S(1)} %get-tuple-element.295), kind=kOutput, calls=%fused_computation.359 | convolution fusion | flops 1032184320 | bytes 35944448 | tf_op jit(solution)/shard_map/qhd,khd->hqk/dot_general | solution.py:543
  232.1 14.3 %fusion.13 = f32[15,512]{1,0:T(8,128)S(1)} fusion(f32[15,512,1024]{2,1,0:T(8,128)} %get-tuple-element.304, f32[15,512]{1,0:T(8,128)S(1)} %get-tuple-element.303), kind=kLoop, calls=%fused_computation.34 | loop fusion | flops 15720960 | bytes 31518720 | tf_op jit(solution)/shard_map/reduce_sum | solution.py:559
  246.6 13.0 %fusion.62 = bf16[512,15,64]{0,2,1:T(8,128)(2,1)S(1)} fusion(bf16[1024,15,64]{0,2,1:T(8,128)(2,1)S(1)} %bitcast.181, f32[15,512,1024]{2,1,0:T(8,128)} %get-tuple-element.304, f32[15,512]{1,0:T(8,128)S(1)} %fusion.13, f32[15,512]{1,0:T(8,128)S(1)} %get-tuple-element.303), kind=kOutput, calls=%fused_computation.148 | convolution fusion | flops 1030717440 | bytes 34467840 | tf_op jit(solution)/shard_map/hqk,khd->qhd/dot_general | solution.py:562
  259.7 14.1 %fusion.12 = f32[15,512]{1,0:T(8,128)S(1)} fusion(f32[15,512,1024]{2,1,0:T(8,128)} %get-tuple-element.306, f32[15,512]{1,0:T(8,128)S(1)} %get-tuple-element.305), kind=kLoop, calls=%fused_computation.33 | loop fusion | flops 15720960 | bytes 31518720 | tf_op jit(solution)/shard_map/reduce_sum | solution.py:559
  273.8 12.3 %fusion.61 = bf16[512,15,64]{0,2,1:T(8,128)(2,1)S(1)} fusion(bf16[1024,15,64]{0,2,1:T(8,128)(2,1)S(1)} %bitcast.182, f32[15,512,1024]{2,1,0:T(8,128)} %get-tuple-element.306, f32[15,512]{1,0:T(8,128)S(1)} %fusion.12, f32[15,512]{1,0:T(8,128)S(1)} %get-tuple-element.305), kind=kOutput, calls=%fused_computation.147 | convolution fusion | flops 1030717440 | bytes 34467840 | tf_op jit(solution)/shard_map/hqk,khd->qhd/dot_general | solution.py:562
  286.4 7.6 multiply_reduce_fusion.10
  295.3 19.5 %fusion.137 = f32[1024,5120]{1,0:T(8,128)} fusion(bf16[960,5120]{1,0:T(8,128)(2,1)} %all-gather.10.cloned.1.call-done, f32[1024,960]{0,1:T(8,128)} %get-tuple-element.308, f32[960]{0:T(1024)S(1)} %bitcast.228, f32[1024]{0:T(1024)S(1)} %get-tuple-element.292), kind=kOutput, calls=%fused_computation.351 | convolution fusion | flops 10069278720 | bytes 34742016 | tf_op jit(solution)/shard_map/dot_general | solution.py:570
  314.8 10.8 multiply_convert_fusion.2
  325.7 9.5 multiply_reduce_fusion.9
  338.7 54.0 %gather_rows.1 = bf16[32,32,1024]{2,1,0:T(8,128)(2,1)} custom-call(bf16[32,1024]{1,0:T(8,128)(2,1)} %maximum_maximum_fusion.x_ref), custom_call_target="tpu_custom_call" | custom-call | tf_op jit(solution)/shard_map/gather_rows/pallas_call | solution.py:94
  394.6 7.5 fusion.153
  407.8 15.5 %gather_stats.1 = f32[32,24,128]{2,1,0:T(8,128)} custom-call(f32[24,128]{1,0:T(8,128)} %pad_maximum_fusion.15.x_ref), custom_call_target="tpu_custom_call" | custom-call | tf_op jit(solution)/shard_map/gather_stats/pallas_call | solution.py:94
  428.4 8.4 fusion.138
  436.9 61.2 %scatter_rows.1 = f32[32,960]{1,0:T(8,128)} custom-call(f32[32,32,960]{2,1,0:T(8,128)} %bitcast.201), custom_call_target="tpu_custom_call" | custom-call | tf_op jit(solution)/shard_map/scatter_rows/pallas_call | solution.py:146
  498.1 5.5 multiply_reduce_fusion.3
  506.3 17.5 %fusion.26 = (bf16[1024,2560]{1,0:T(8,128)(2,1)}, bf16[1024,2560]{1,0:T(8,128)(2,1)}) fusion(f32[1024,5120]{1,0:T(8,128)} %fusion.137, bf16[1024,960]{0,1:T(8,128)(2,1)S(1)} %fusion.58, bf16[2560,960]{1,0:T(8,128)(2,1)} %all-gather.12.cloned.1.call-done), kind=kOutput, calls=%fused_computation.47 | convolution fusion | flops 5072486400 | bytes 38338560 | tf_op jit(solution)/shard_map/dot_general | solution.py:279
  523.8 19.0 %multiply_reduce_fusion.4 = (f32[960]{0:T(1024)}, f32[1024]{0:T(1024)S(1)}, f32[1024,960]{0,1:T(8,128)}) fusion(f32[1024,960]{0,1:T(8,128)} %get-tuple-element.308, f32[1024]{0:T(1024)S(1)} %get-tuple-element.292, f32[960]{0:T(1024)S(1)} %bitcast.229, bf16[960,5120]{1,0:T(8,128)(2,1)} %all-gather.10.cloned.1.call-done, ...), kind=kOutput, calls=%fused_computation.84 | convolution fusion | flops 10093197312 | bytes 28196352 | tf_op jit(solution)/shard_map/dot_general | solution.py:279
  558.2 14.6 %fusion.16 = f32[15,64,1024]{2,1,0:T(8,128)} fusion(bf16[512,15,64]{0,2,1:T(8,128)(2,1)S(1)} %bitcast.197, f32[15,512,1024]{2,1,0:T(8,128)} %get-tuple-element.304, f32[15,512]{1,0:T(8,128)S(1)} %copy-done.40), kind=kOutput, calls=%fused_computation.37 | convolution fusion | flops 1022361600 | bytes 36403200 | tf_op jit(solution)/shard_map/hqk,qhd->khd/dot_general | solution.py:664
  572.9 23.9 %multiply_reduce_fusion = (f32[15,512]{1,0:T(8,128)S(1)}, f32[15,512,1024]{2,1,0:T(8,128)}) fusion(f32[15,512,1024]{2,1,0:T(8,128)} %get-tuple-element.304, f32[15,512]{1,0:T(8,128)S(1)} %copy-done.40, bf16[512,15,64]{0,2,1:T(8,128)(2,1)S(1)} %bitcast.198, bf16[1024,15,64]{0,2,1:T(8,128)(2,1)S(1)} %bitcast.183), kind=kOutput, calls=%fused_computation.22 | convolution fusion | flops 1030218240 | bytes 65925120 | tf_op jit(solution)/shard_map/qhd,khd->hqk/dot_general | solution.py:670
  596.9 24.5 %multiply_reduce_fusion.1 = (f32[15,512]{1,0:T(8,128)S(1)}, f32[15,512,1024]{2,1,0:T(8,128)}) fusion(f32[15,512,1024]{2,1,0:T(8,128)} %get-tuple-element.306, f32[15,512]{1,0:T(8,128)S(1)} %copy-done.41, bf16[512,15,64]{0,2,1:T(8,128)(2,1)S(1)} %bitcast.195, bf16[1024,15,64]{0,2,1:T(8,128)(2,1)S(1)} %bitcast.184), kind=kOutput, calls=%fused_computation.25 | convolution fusion | flops 1030218240 | bytes 65925120 | tf_op jit(solution)/shard_map/qhd,khd->hqk/dot_general | solution.py:670
  621.4 16.3 %fusion.51 = f32[15,64,1024]{2,1,0:T(8,128)} fusion(f32[15,64,1024]{2,1,0:T(8,128)} %fusion.16, bf16[512,15,64]{0,2,1:T(8,128)(2,1)S(1)} %bitcast.196, f32[15,512,1024]{2,1,0:T(8,128)} %get-tuple-element.306, f32[15,512]{1,0:T(8,128)S(1)} %copy-done.41), kind=kOutput, calls=%fused_computation.134 | convolution fusion | flops 1023344640 | bytes 40335360 | tf_op jit(solution)/shard_map/hqk,qhd->khd/dot_general | solution.py:664
  637.7 26.7 %multiply_convert_fusion.1 = bf16[15,512,1024]{2,1,0:T(8,128)(2,1)} fusion(f32[15,512,1024]{2,1,0:T(8,128)} %get-tuple-element.316, f32[15,512,1024]{2,1,0:T(8,128)} %get-tuple-element.306, f32[15,512]{1,0:T(8,128)S(1)} %get-tuple-element.315, f32[15,512]{1,0:T(8,128)S(1)} %copy-done.41), kind=kLoop, calls=%fused_computation.24 | loop fusion | flops 31457280 | bytes 78704640 | tf_op jit(solution)/shard_map/convert_element_type | solution.py:675
  664.4 10.2 fusion.133
  674.6 26.3 %multiply_convert_fusion = bf16[15,512,1024]{2,1,0:T(8,128)(2,1)} fusion(f32[15,512,1024]{2,1,0:T(8,128)} %get-tuple-element.318, f32[15,512,1024]{2,1,0:T(8,128)} %get-tuple-element.304, f32[15,512]{1,0:T(8,128)S(1)} %get-tuple-element.317, f32[15,512]{1,0:T(8,128)S(1)} %copy-done.40), kind=kLoop, calls=%fused_computation.21 | loop fusion | flops 31457280 | bytes 78704640 | tf_op jit(solution)/shard_map/convert_element_type | solution.py:675
  700.9 11.4 add_multiply_fusion
  712.3 11.6 %multiply_bitcast_fusion.1 = f32[512,15,64]{0,2,1:T(8,128)} fusion(bf16[1024,15,64]{0,2,1:T(8,128)(2,1)S(1)} %bitcast.177, bf16[15,512,1024]{2,1,0:T(8,128)(2,1)} %multiply_convert_fusion.1), kind=kOutput, calls=%fused_computation.126 | convolution fusion | flops 1007124480 | bytes 19660800 | tf_op jit(solution)/shard_map/hqk,khd->qhd/dot_general | solution.py:677
  730.5 11.6 %multiply_bitcast_fusion = f32[512,15,64]{0,2,1:T(8,128)} fusion(bf16[1024,15,64]{0,2,1:T(8,128)(2,1)S(1)} %bitcast.178, bf16[15,512,1024]{2,1,0:T(8,128)(2,1)} %multiply_convert_fusion), kind=kOutput, calls=%fused_computation.125 | convolution fusion | flops 1007124480 | bytes 19660800 | tf_op jit(solution)/shard_map/hqk,khd->qhd/dot_general | solution.py:677
  747.7 7.2 convolution_convert_fusion.4
  755.0 9.9 convolution_convert_fusion.2
  765.6 17.7 %convolution_convert_fusion.1 = bf16[960,5120]{1,0:T(8,128)(2,1)} fusion(bf16[1024,2560]{1,0:T(8,128)(2,1)} %get-tuple-element.264, bf16[1024,2560]{1,0:T(8,128)(2,1)} %get-tuple-element.263, f32[1024,960]{0,1:T(8,128)} %get-tuple-element.308, f32[960]{0:T(1024)S(1)} %bitcast.231, f32[1024]{0:T(1024)S(1)} %copy-done.63), kind=kOutput, calls=%fused_computation.56 | convolution fusion | flops 10095165440 | bytes 24256256 | tf_op jit(solution)/shard_map/dot_general | solution.py:285
  784.8 8.3 multiply_reduce_fusion.5
  793.3 5.3 add_convert_fusion.2
  811.1 77.7 %deal_rows.5 = (bf16[32,48,960]{2,1,0:T(8,128)(2,1)}, f32[32,24,128]{2,1,0:T(8,128)}) custom-call(bf16[32,48,960]{2,1,0:T(8,128)(2,1)} %bitcast.194, f32[24,128]{1,0:T(8,128)S(1)} %pad_bitcast_fusion.note_ref), custom_call_target="tpu_custom_call" | custom-call | tf_op jit(solution)/shard_map/deal_rows/pallas_call | solution.py:238
  888.8 7.2 fusion.54
  896.1 7.5 bitcast_add_fusion.1
  903.5 84.5 %reduce-scatter.9.cloned.1.call-done = bf16[120,5120]{1,0:T(8,128)(2,1)} async-done(((bf16[960,5120]{1,0:T(8,128)(2,1)}), bf16[120,5120]{1,0:T(8,128)(2,1)}) %reduce-scatter.9.cloned.1.call-update) | async-done | bytes 1228816 | tf_op jit(solution)/shard_map/reduce_scatter | solution.py:736
  997.0 95.2 %all-reduce.5.cloned.1.call-done = (bf16[120,1600]{1,0:T(8,128)(2,1)}, bf16[120,960]{1,0:T(8,128)(2,1)}, bf16[120,5120]{1,0:T(8,128)(2,1)}, bf16[320,960]{1,0:T(8,128)(2,1)}) async-done(((bf16[120,1600]{1,0:T(8,128)(2,1)}, bf16[120,960]{1,0:T(8,128)(2,1)}, bf16[120,5120]{1,0:T(8,128)(2,1)}, bf16[320,960]{1,0:T(8,128)(2,1)}), (bf16[120,1600]{1,0:T(8,128)(2,1)}, bf16[120,960]{1,0:T(8,128)(2,1)}, ...) | async-done | bytes 2457616 | tf_op jit(solution)/shard_map/psum | solution.py:735
  1104.7 15.9 %gather_squares.1 = f32[32,8,128]{2,1,0:T(8,128)} custom-call(f32[8,128]{1,0:T(8,128)} %broadcast_in_dim.246.x_ref), custom_call_target="tpu_custom_call" | custom-call | tf_op jit(solution)/shard_map/gather_squares/pallas_call | solution.py:94
  1138.5 10.7 multiply_add_fusion.1
  (362 shorter events, 142.2 us)
Async XLA Ops:
  7.2 186.6 %all-gather.6.cloned.1.call-start = ((), (), s32[]{:S(2)}) async-start(), calls=%async_computation.4 | async-start | bytes 3594240 | tf_op jit(solution)/shard_map/all_gather | solution.py:371
  9.4 277.1 %all-gather.8.cloned.1.call-start = ((), (), s32[]{:S(2)}) async-start(), calls=%async_computation.5 | async-start | bytes 2211840 | tf_op jit(solution)/shard_map/all_gather | solution.py:372
  11.2 25.6 %copy-start.88 = (s32[64]{0:T(128)S(1)}, s32[64]{0:T(128)}, u32[]{:S(2)}) copy-start(s32[64]{0:T(128)} %constant.349.clone) | copy-start | bytes 772
  11.2 36.4 %copy-start.94 = (s32[64]{0:T(128)S(1)}, s32[64]{0:T(128)}, u32[]{:S(2)}) copy-start(s32[64]{0:T(128)} %constant.356) | copy-start | bytes 772
  11.2 284.1 %all-gather.10.cloned.1.call-start = ((), (), s32[]{:S(2)}) async-start(), calls=%async_computation.6 | async-start | bytes 11059200 | tf_op jit(solution)/shard_map/all_gather | solution.py:373
  12.5 313.2 %all-gather.12.cloned.1.call-start = ((), (), s32[]{:S(2)}) async-start(), calls=%async_computation.7 | async-start | bytes 5898240 | tf_op jit(solution)/shard_map/all_gather | solution.py:374
  14.8 52.7 %copy-start.75 = (f32[3,120]{1,0:T(4,128)S(1)}, f32[3,120]{1,0:T(4,128)}, u32[]{:S(2)}) copy-start(f32[3,120]{1,0:T(4,128)} %param.35) | copy-start | bytes 4324
  14.8 888.7 %reduce-scatter.7.cloned.1.call-start = ((), (), s32[]{:S(2)}) async-start(), calls=%async_computation.8 | async-start | bytes 2211840 | tf_op jit(solution)/shard_map/reduce_scatter | solution.py:736
  14.9 69.9 %copy-start.77 = (s32[32]{0:T(128)}, s32[32]{0:T(128)S(1)}, u32[]{:S(2)}) copy-start(s32[32]{0:T(128)S(1)} %iota_add_fusion) | copy-start | bytes 388
  14.9 69.9 %copy-start.86 = (f32[48]{0:T(128)}, f32[48]{0:T(128)S(1)}, u32[]{:S(2)}) copy-start(f32[48]{0:T(128)S(1)} %add_convert_fusion.7) | copy-start | bytes 580
  42.2 42.6 %copy-start.69 = (pred[1024]{0:T(1024)(128)(4,1)}, pred[1024]{0:T(1024)(128)(4,1)S(1)}, u32[]{:S(2)}) copy-start(pred[1024]{0:T(1024)(128)(4,1)S(1)} %get-tuple-element.258) | copy-start | bytes 3076
  45.7 131.0 %copy-start.79 = (s32[1024]{0:T(1024)}, s32[1024]{0:T(1024)S(1)}, u32[]{:S(2)}) copy-start(s32[1024]{0:T(1024)S(1)} %get-tuple-element.299) | copy-start | bytes 12292
  67.3 17.5 %copy-start.44 = (f32[32,1536]{1,0:T(8,128)}, f32[32,1536]{1,0:T(8,128)S(1)}, u32[]{:S(2)}) copy-start(f32[32,1536]{1,0:T(8,128)S(1)} %copy_bitcast_fusion.2) | copy-start | bytes 589828
  67.5 17.3 %copy-start.71 = (s32[1024]{0:T(1024)}, s32[1024]{0:T(1024)S(1)}, u32[]{:S(2)}) copy-start(s32[1024]{0:T(1024)S(1)} %iota.102) | copy-start | bytes 12292
  77.6 116.2 %copy-start.64 = (f32[1,960]{1,0:T(1,128)}, f32[1,960]{1,0:T(1,128)S(1)}, u32[]{:S(2)}) copy-start(f32[1,960]{1,0:T(1,128)S(1)} %get-tuple-element.283) | copy-start | bytes 11524
  184.5 16.4 %copy-start.6 = (f32[32,12,128]{2,1,0:T(8,128)}, f32[32,12,128]{2,1,0:T(8,128)S(1)}, u32[]{:S(2)}) copy-start(f32[32,12,128]{2,1,0:T(8,128)S(1)} %get-tuple-element.494) | copy-start | bytes 589828
  184.5 16.4 %copy-start.47 = (s32[1024]{0:T(1024)}, s32[1024]{0:T(1024)S(1)}, u32[]{:S(2)}) copy-start(s32[1024]{0:T(1024)S(1)} %get-tuple-element.522) | copy-start | bytes 12292
  184.5 16.4 %copy-start.49 = (s32[1024]{0:T(1024)}, s32[1024]{0:T(1024)S(1)}, u32[]{:S(2)}) copy-start(s32[1024]{0:T(1024)S(1)} %get-tuple-element.523) | copy-start | bytes 12292
  204.3 14.7 %copy-start.10 = (bf16[1024,15,32]{0,2,1:T(8,128)(2,1)}, bf16[1024,15,32]{0,2,1:T(8,128)(2,1)S(1)}, u32[]{:S(2)}) copy-start(bf16[1024,15,32]{0,2,1:T(8,128)(2,1)S(1)} %get-tuple-element.267) | copy-start | bytes 2949124
  204.3 14.7 %copy-start.12 = (bf16[1024,15,32]{0,2,1:T(8,128)(2,1)}, bf16[1024,15,32]{0,2,1:T(8,128)(2,1)S(1)}, u32[]{:S(2)}) copy-start(bf16[1024,15,32]{0,2,1:T(8,128)(2,1)S(1)} %get-tuple-element.268) | copy-start | bytes 2949124
  246.6 27.2 %copy-start.8 = (bf16[1024,5,3,64]{0,3,2,1:T(8,128)(2,1)}, bf16[1024,5,3,64]{0,3,2,1:T(8,128)(2,1)S(1)}, u32[]{:S(2)}) copy-start(bf16[1024,5,3,64]{0,3,2,1:T(8,128)(2,1)S(1)} %broadcast_in_dim.147) | copy-start | bytes 5898244
  294.0 248.7 %copy-start.62 = (f32[1024]{0:T(1024)}, f32[1024]{0:T(1024)S(1)}, u32[]{:S(2)}) copy-start(f32[1024]{0:T(1024)S(1)} %get-tuple-element.292) | copy-start | bytes 12292
  335.2 59.5 %copy-start.25 = (bf16[1536,960]{1,0:T(8,128)(2,1)S(1)}, bf16[1536,960]{1,0:T(8,128)(2,1)}, u32[]{:S(2)}) copy-start(bf16[1536,960]{1,0:T(8,128)(2,1)} %get-tuple-element.505) | copy-start | bytes 8847364
  403.4 25.0 %copy-start.59 = (s32[1024,1]{0,1:T(1,128)}, s32[1024,1]{0,1:T(1,128)S(1)}, u32[]{:S(2)}) copy-start(s32[1024,1]{0,1:T(1,128)S(1)} %add_subtract_fusion) | copy-start | bytes 12292
  506.3 17.5 %copy-start.29 = (bf16[1024,960]{0,1:T(8,128)(2,1)}, bf16[1024,960]{0,1:T(8,128)(2,1)S(1)}, u32[]{:S(2)}) copy-start(bf16[1024,960]{0,1:T(8,128)(2,1)S(1)} %fusion.58) | copy-start | bytes 5898244
  523.8 19.0 %copy-start.5 = (f32[1024,960]{0,1:T(8,128)S(1)}, f32[1024,960]{0,1:T(8,128)}, u32[]{:S(2)}) copy-start(f32[1024,960]{0,1:T(8,128)} %copy-done.4) | copy-start | bytes 11796484
  558.2 14.6 %copy-start.9 = (bf16[1024,5,3,64]{0,3,2,1:T(8,128)(2,1)S(1)}, bf16[1024,5,3,64]{0,3,2,1:T(8,128)(2,1)}, u32[]{:S(2)}) copy-start(bf16[1024,5,3,64]{0,3,2,1:T(8,128)(2,1)} %copy-done.8) | copy-start | bytes 5898244
  572.9 24.0 %copy-start.41 = (f32[15,512]{1,0:T(8,128)S(1)}, f32[15,512]{1,0:T(8,128)}, u32[]{:S(2)}) copy-start(f32[15,512]{1,0:T(8,128)} %log_add_fusion.1) | copy-start | bytes 92164
  596.8 306.7 %reduce-scatter.13.cloned.1.call-start = ((), (), s32[]{:S(2)}) async-start(), calls=%async_computation.11 | async-start | bytes 3594240
  637.7 26.7 %copy-start.11 = (bf16[1024,15,32]{0,2,1:T(8,128)(2,1)S(1)}, bf16[1024,15,32]{0,2,1:T(8,128)(2,1)}, u32[]{:S(2)}) copy-start(bf16[1024,15,32]{0,2,1:T(8,128)(2,1)} %copy-done.10) | copy-start | bytes 2949124
  637.7 26.7 %copy-start.13 = (bf16[1024,15,32]{0,2,1:T(8,128)(2,1)S(1)}, bf16[1024,15,32]{0,2,1:T(8,128)(2,1)}, u32[]{:S(2)}) copy-start(bf16[1024,15,32]{0,2,1:T(8,128)(2,1)} %copy-done.12) | copy-start | bytes 2949124
  754.9 148.7 %reduce-scatter.11.cloned.1.call-start = ((), (), s32[]{:S(2)}) async-start(), calls=%async_computation.10 | async-start | bytes 5898240 | tf_op jit(solution)/shard_map/reduce_scatter | solution.py:736
  764.9 223.1 %reduce-scatter.9.cloned.1.call-start = ((), (), s32[]{:S(2)}) async-start(), calls=%async_computation.9 | async-start | bytes 11059200 | tf_op jit(solution)/shard_map/reduce_scatter | solution.py:736
  783.3 308.9 %all-reduce.5.cloned.1.call-start = ((), (), s32[]{:S(2)}) async-start(), calls=%async_computation.12 | async-start | bytes 5058560 | tf_op jit(solution)/shard_map/psum | solution.py:735
  806.2 82.5 %copy-start.23 = (bf16[32,32,1024]{2,1,0:T(8,128)(2,1)S(1)}, bf16[32,32,1024]{2,1,0:T(8,128)(2,1)}, u32[]{:S(2)}) copy-start(bf16[32,32,1024]{2,1,0:T(8,128)(2,1)} %gather_rows.1) | copy-start | bytes 6291460
  806.2 82.5 %copy-start.60 = (s32[1024,1]{0,1:T(1,128)S(1)}, s32[1024,1]{0,1:T(1,128)}, u32[]{:S(2)}) copy-start(s32[1024,1]{0,1:T(1,128)} %copy-done.59) | copy-start | bytes 12292
  806.2 82.5 %copy-start.83 = (f32[1024]{0:T(1024)S(1)}, f32[1024]{0:T(1024)}, u32[]{:S(2)}) copy-start(f32[1024]{0:T(1024)} %copy-done.82) | copy-start | bytes 12292
  896.0 92.0 %copy-start.7 = (f32[32,12,128]{2,1,0:T(8,128)S(1)}, f32[32,12,128]{2,1,0:T(8,128)}, u32[]{:S(2)}) copy-start(f32[32,12,128]{2,1,0:T(8,128)} %copy-done.6) | copy-start | bytes 589828
  896.0 92.0 %copy-start.48 = (s32[1024]{0:T(1024)S(1)}, s32[1024]{0:T(1024)}, u32[]{:S(2)}) copy-start(s32[1024]{0:T(1024)} %copy-done.47) | copy-start | bytes 12292
  896.0 92.0 %copy-start.50 = (s32[1024]{0:T(1024)S(1)}, s32[1024]{0:T(1024)}, u32[]{:S(2)}) copy-start(s32[1024]{0:T(1024)} %copy-done.49) | copy-start | bytes 12292
  992.1 130.8 %copy-start.76 = (f32[3,120]{1,0:T(4,128)S(1)}, f32[3,120]{1,0:T(4,128)}, u32[]{:S(2)}) copy-start(f32[3,120]{1,0:T(4,128)} %param.35) | copy-start | bytes 4324
  992.1 130.8 %copy-start.84 = (f32[3,120]{1,0:T(4,128)S(1)}, f32[3,120]{1,0:T(4,128)}, u32[]{:S(2)}) copy-start(f32[3,120]{1,0:T(4,128)} %param.41) | copy-start | bytes 4324
  992.1 130.8 %copy-start.85 = (f32[3,120]{1,0:T(4,128)S(1)}, f32[3,120]{1,0:T(4,128)}, u32[]{:S(2)}) copy-start(f32[3,120]{1,0:T(4,128)} %param.47) | copy-start | bytes 4324
  992.1 131.5 %copy-start.35 = (f32[120,960]{1,0:T(8,128)S(1)}, f32[120,960]{1,0:T(8,128)}, u32[]{:S(2)}) copy-start(f32[120,960]{1,0:T(8,128)} %param.32) | copy-start | bytes 1382404
  997.0 129.5 %copy-start.24 = (f32[120,1600]{1,0:T(8,128)S(1)}, f32[120,1600]{1,0:T(8,128)}, u32[]{:S(2)}) copy-start(f32[120,1600]{1,0:T(8,128)} %param.31) | copy-start | bytes 2304004
  997.0 129.5 %copy-start.42 = (f32[120,1600]{1,0:T(8,128)S(1)}, f32[120,1600]{1,0:T(8,128)}, u32[]{:S(2)}) copy-start(f32[120,1600]{1,0:T(8,128)} %param.37) | copy-start | bytes 2304004
  997.0 129.5 %copy-start.43 = (f32[120,1600]{1,0:T(8,128)S(1)}, f32[120,1600]{1,0:T(8,128)}, u32[]{:S(2)}) copy-start(f32[120,1600]{1,0:T(8,128)} %param.43) | copy-start | bytes 2304004
  1092.2 34.3 %copy-start.36 = (bf16[120,1600]{1,0:T(8,128)(2,1)S(1)}, bf16[120,1600]{1,0:T(8,128)(2,1)}, u32[]{:S(2)}) copy-start(bf16[120,1600]{1,0:T(8,128)(2,1)} %get-tuple-element.233) | copy-start | bytes 1152004
  (62 other events, 357.7 us)
Sparse Core Ops, SparseCore 0:
  10.5 35.5 all-gather.5
  48.5 27.6 all-gather.7
  78.7 92.7 all-gather.9
  173.8 48.5 all-gather.11
  596.9 38.4 reduce-scatter.6
  755.0 43.8 reduce-scatter.12
  802.3 90.4 reduce-scatter.10
  896.4 91.6 reduce-scatter.8
  990.7 101.4 all-reduce.4
